TPU v7x, 32 devices: a 4x4x1 block of a 4x4x8 slice. The times are simulated.
32 devices in a mesh: part: 1 (over z), data: 4 (over y), stage: 8 (over x, core).
Axes of the slice: x: 4, y: 4, z: 1, core: 2. Of those that a mesh axis runs over, the one named last changes fastest.
The devices are a block of a 4x4x8 slice.
Arguments:
- x: bfloat16 [32, 256, 768], P(('part', 'data'))
- g: bfloat16 [32, 256, 768], P(('part', 'data'))
- w_in: bfloat16 [2, 8, 768, 3072], P(None, 'stage')
- w_out: bfloat16 [2, 8, 3072, 768], P(None, 'stage')
Outputs:
- output 1: bfloat16 [32, 256, 768], P(('part', 'data'))
- output 2: bfloat16 [32, 256, 768], P(('part', 'data'))
- output 3: float32 [2, 8, 768, 3072], P('part', 'stage')
- output 4: float32 [2, 8, 3072, 768], P('part', 'stage')
All inputs are finite; a program needn't handle non-finite values.
Results may differ from a plain program's by a relative error of at most 0.02.
Values are sent between devices in bfloat16 or wider.
A program may use at most 768 MiB of HBM per device.

v0:
```python
import functools
import jax
import jax.numpy as jnp
from jax import lax
from jax.sharding import PartitionSpec as P


def layer_forward(h_in, w_first, w_second):
    pre_act = jnp.dot(h_in, w_first, preferred_element_type=jnp.float32)
    hidden = jax.nn.gelu(pre_act, approximate=True).astype(jnp.bfloat16)
    delta_out = jnp.dot(hidden, w_second, preferred_element_type=jnp.float32)
    return (h_in.astype(jnp.float32) + delta_out).astype(jnp.bfloat16), pre_act


def layer_backward(h_in, pre_act, g_next, w_first, w_second):
    gelu_val, gelu_pull = jax.vjp(functools.partial(jax.nn.gelu, approximate=True), pre_act)
    hidden = gelu_val.astype(jnp.bfloat16)
    grad_second = jnp.einsum('tf,td->fd', hidden, g_next, preferred_element_type=jnp.float32)
    grad_hidden = jnp.einsum('td,fd->tf', g_next, w_second, preferred_element_type=jnp.float32)
    grad_pre = gelu_pull(grad_hidden)[0].astype(jnp.bfloat16)
    grad_first = jnp.einsum('td,tf->df', h_in, grad_pre, preferred_element_type=jnp.float32)
    grad_prev = jnp.einsum('tf,df->td', grad_pre, w_first, preferred_element_type=jnp.float32)
    g_prev = (g_next.astype(jnp.float32) + grad_prev).astype(jnp.bfloat16)
    return g_prev, grad_first, grad_second


def pick_row(stacked, row_idx):
    return lax.dynamic_index_in_dim(stacked, row_idx, 0, keepdims=False)


def put_row(stacked, row_val, row_idx):
    return lax.dynamic_update_index_in_dim(stacked, row_val, row_idx, 0)


def solution(mesh):
    stages = mesh.shape['stage']
    to_next = [(source_idx, (source_idx + 1) % stages) for source_idx in range(stages)]
    to_prev = [(source_idx, (source_idx - 1) % stages) for source_idx in range(stages)]

    def local_fn(x, g, w_in, w_out):
        first_loc = w_in[:, 0]
        second_loc = w_out[:, 0]
        dev_layers, model_dim, hidden_dim = first_loc.shape
        micro_count, tokens = x.shape[0], x.shape[1]
        unit_count = dev_layers * micro_count
        span_size = dev_layers * stages
        tick_count = unit_count + stages - 1
        stage_idx = lax.axis_index('stage')
        is_first = stage_idx == 0
        is_last = stage_idx == stages - 1

        def fwd_tick(tick_idx, loop_state):
            incoming, h_saved, pre_saved, y_buf = loop_state
            unit_raw = tick_idx - stage_idx
            active = (unit_raw >= 0) & (unit_raw < unit_count)
            unit_idx = jnp.clip(unit_raw, 0, unit_count - 1)
            group_idx = unit_idx // span_size
            within = unit_idx % span_size
            layer_idx = within // stages
            micro_idx = group_idx * stages + within % stages

            def run_unit(buffers):
                h_saved, pre_saved, y_buf = buffers
                h_in = jnp.where(is_first & (layer_idx == 0), pick_row(x, micro_idx), incoming)
                h_out, pre_act = layer_forward(h_in, pick_row(first_loc, layer_idx), pick_row(second_loc, layer_idx))
                h_saved = put_row(h_saved, h_in, unit_idx)
                pre_saved = put_row(pre_saved, pre_act, unit_idx)
                y_new = jnp.where(is_last & (layer_idx == dev_layers - 1), h_out, pick_row(y_buf, micro_idx))
                y_buf = put_row(y_buf, y_new, micro_idx)
                return h_out, h_saved, pre_saved, y_buf

            def skip_unit(buffers):
                return (jnp.zeros((tokens, model_dim), jnp.bfloat16),) + buffers

            h_out, h_saved, pre_saved, y_buf = lax.cond(active, run_unit, skip_unit, (h_saved, pre_saved, y_buf))
            return lax.ppermute(h_out, 'stage', to_next), h_saved, pre_saved, y_buf

        fwd_init = (jnp.zeros((tokens, model_dim), jnp.bfloat16), jnp.zeros((unit_count, tokens, model_dim), jnp.bfloat16), jnp.zeros((unit_count, tokens, hidden_dim), jnp.float32), jnp.zeros_like(x))
        last_sent, h_saved, pre_saved, y_buf = lax.fori_loop(0, tick_count, fwd_tick, fwd_init)

        def bwd_tick(tick_idx, loop_state):
            incoming, acc_first, acc_second, dx_buf = loop_state
            unit_raw = tick_idx - (stages - 1 - stage_idx)
            active = (unit_raw >= 0) & (unit_raw < unit_count)
            unit_idx = jnp.clip(unit_raw, 0, unit_count - 1)
            group_idx = unit_idx // span_size
            within = unit_idx % span_size
            layer_idx = dev_layers - 1 - within // stages
            lane_idx = within % stages
            micro_idx = group_idx * stages + lane_idx
            saved_idx = group_idx * span_size + layer_idx * stages + lane_idx

            def run_unit(buffers):
                acc_first, acc_second, dx_buf = buffers
                g_next = jnp.where(is_last & (layer_idx == dev_layers - 1), pick_row(g, micro_idx), incoming)
                g_prev, grad_first, grad_second = layer_backward(pick_row(h_saved, saved_idx), pick_row(pre_saved, saved_idx), g_next, pick_row(first_loc, layer_idx), pick_row(second_loc, layer_idx))
                acc_first = put_row(acc_first, pick_row(acc_first, layer_idx) + grad_first, layer_idx)
                acc_second = put_row(acc_second, pick_row(acc_second, layer_idx) + grad_second, layer_idx)
                dx_new = jnp.where(is_first & (layer_idx == 0), g_prev, pick_row(dx_buf, micro_idx))
                dx_buf = put_row(dx_buf, dx_new, micro_idx)
                return g_prev, acc_first, acc_second, dx_buf

            def skip_unit(buffers):
                return (jnp.zeros((tokens, model_dim), jnp.bfloat16),) + buffers

            g_prev, acc_first, acc_second, dx_buf = lax.cond(active, run_unit, skip_unit, (acc_first, acc_second, dx_buf))
            return lax.ppermute(g_prev, 'stage', to_prev), acc_first, acc_second, dx_buf

        bwd_init = (jnp.zeros((tokens, model_dim), jnp.bfloat16), jnp.zeros((dev_layers, model_dim, hidden_dim), jnp.float32), jnp.zeros((dev_layers, hidden_dim, model_dim), jnp.float32), jnp.zeros_like(x))
        last_grad, acc_first, acc_second, dx_buf = lax.fori_loop(0, tick_count, bwd_tick, bwd_init)
        y_full = lax.psum(jnp.where(is_last, y_buf, jnp.zeros_like(y_buf)), 'stage')
        dx_full = lax.psum(jnp.where(is_first, dx_buf, jnp.zeros_like(dx_buf)), 'stage')
        grad_first = lax.psum(acc_first, 'data')
        grad_second = lax.psum(acc_second, 'data')
        return y_full, dx_full, grad_first[:, None], grad_second[:, None]

    spec_rows = P(('part', 'data'))
    spec_weights = P(None, 'stage')
    spec_grads = P('part', 'stage')
    return jax.shard_map(local_fn, mesh=mesh, in_specs=(spec_rows, spec_rows, spec_weights, spec_weights), out_specs=(spec_rows, spec_rows, spec_grads, spec_grads), check_vma=False)
```

profile of v0, /device:TPU:96, one launch (start us, length us, event | category | flops | bytes accessed | tf_op | source)
XLA Modules:
  0.0 2209.4 jit_solution(7770014343645294473)
XLA Ops:
  11.2 16.3 broadcast_in_dim.66
  27.7 437.0 %while.44 = (s32[]{:T(128)}, bf16[256,768]{1,0:T(8,128)(2,1)}, bf16[16,256,768]{2,1,0:T(8,128)(2,1)}, f32[16,256,3072]{2,1,0:T(8,128)}, bf16[8,256,768]{2,1,0:T(...) while((s32[]{:T(128)}, bf16[256,768]{1,0:T(8,128)(2,1)}, ...), condition=%wide.region_3.4_spmd, body=%wide.region_0.3_spmd.sunk | while | flops 2423980032 | bytes 65668140 | solution.py:79
  27.8 10.8 conditional.4
  47.7 10.7 conditional.4
  107.4 10.7 conditional.4
  127.3 10.7 conditional.4
  186.9 10.8 conditional.4
  206.9 10.8 conditional.4
  226.9 10.8 conditional.4
  246.9 10.9 conditional.4
  266.9 10.8 conditional.4
  286.9 10.8 conditional.4
  306.9 10.8 conditional.4
  326.9 10.9 conditional.4
  351.1 11.4 collective-permute-done
  364.0 14.8 collective-permute-done
  380.3 14.8 collective-permute-done
  396.6 14.7 collective-permute-done
  412.9 14.8 collective-permute-done
  429.2 15.9 collective-permute-done
  446.6 17.3 collective-permute-done
  485.8 971.6 %while.45 = (s32[]{:T(128)}, bf16[256,768]{1,0:T(8,128)(2,1)S(1)}, f32[2,768,3072]{2,1,0:T(8,128)}, f32[2,3072,768]{2,1,0:T(8,128)}, bf16[8,256,768]{2,1,0:T(8,1...) while((s32[]{:T(128)}, bf16[256,768]{1,0:T(8,128)(2,1)S(1)}, ...), condition=%wide.region_8.9_spmd, body=%wide.region_5.8_spmd.sunk | while | flops 4860346368 | bytes 132121704 | solution.py:110
  486.6 33.4 %collective-permute-start.1 = (bf16[256,768]{1,0:T(8,128)(2,1)}, bf16[256,768]{1,0:T(8,128)(2,1)S(1)}, u32[]{:S(2)}, u32[]{:S(2)}) collective-permute-start(bf16[256,768]{1,0:T(8,128)(2,1)} %get-tuple-element.1689), channel_id=1, source_target_pairs={{0,7},{1,0},{2,1},{3,2},{4,3},{5,4},{6,5},{7,6},{8,15},{9,8},{10,9... | collective-permute-start | bytes 1179656 | tf_op jit(solution)/shard_map/while/body/eval_jaxpr/ppermute | solution.py:107
  526.1 37.3 %collective-permute-start.1 = (bf16[256,768]{1,0:T(8,128)(2,1)}, bf16[256,768]{1,0:T(8,128)(2,1)S(1)}, u32[]{:S(2)}, u32[]{:S(2)}) collective-permute-start(bf16[256,768]{1,0:T(8,128)(2,1)} %get-tuple-element.1689), channel_id=1, source_target_pairs={{0,7},{1,0},{2,1},{3,2},{4,3},{5,4},{6,5},{7,6},{8,15},{9,8},{10,9... | collective-permute-start | bytes 1179656 | tf_op jit(solution)/shard_map/while/body/eval_jaxpr/ppermute | solution.py:107
  569.5 37.3 %collective-permute-start.1 = (bf16[256,768]{1,0:T(8,128)(2,1)}, bf16[256,768]{1,0:T(8,128)(2,1)S(1)}, u32[]{:S(2)}, u32[]{:S(2)}) collective-permute-start(bf16[256,768]{1,0:T(8,128)(2,1)} %get-tuple-element.1689), channel_id=1, source_target_pairs={{0,7},{1,0},{2,1},{3,2},{4,3},{5,4},{6,5},{7,6},{8,15},{9,8},{10,9... | collective-permute-start | bytes 1179656 | tf_op jit(solution)/shard_map/while/body/eval_jaxpr/ppermute | solution.py:107
  612.9 37.3 %collective-permute-start.1 = (bf16[256,768]{1,0:T(8,128)(2,1)}, bf16[256,768]{1,0:T(8,128)(2,1)S(1)}, u32[]{:S(2)}, u32[]{:S(2)}) collective-permute-start(bf16[256,768]{1,0:T(8,128)(2,1)} %get-tuple-element.1689), channel_id=1, source_target_pairs={{0,7},{1,0},{2,1},{3,2},{4,3},{5,4},{6,5},{7,6},{8,15},{9,8},{10,9... | collective-permute-start | bytes 1179656 | tf_op jit(solution)/shard_map/while/body/eval_jaxpr/ppermute | solution.py:107
  656.3 37.3 %collective-permute-start.1 = (bf16[256,768]{1,0:T(8,128)(2,1)}, bf16[256,768]{1,0:T(8,128)(2,1)S(1)}, u32[]{:S(2)}, u32[]{:S(2)}) collective-permute-start(bf16[256,768]{1,0:T(8,128)(2,1)} %get-tuple-element.1689), channel_id=1, source_target_pairs={{0,7},{1,0},{2,1},{3,2},{4,3},{5,4},{6,5},{7,6},{8,15},{9,8},{10,9... | collective-permute-start | bytes 1179656 | tf_op jit(solution)/shard_map/while/body/eval_jaxpr/ppermute | solution.py:107
  699.7 37.3 %collective-permute-start.1 = (bf16[256,768]{1,0:T(8,128)(2,1)}, bf16[256,768]{1,0:T(8,128)(2,1)S(1)}, u32[]{:S(2)}, u32[]{:S(2)}) collective-permute-start(bf16[256,768]{1,0:T(8,128)(2,1)} %get-tuple-element.1689), channel_id=1, source_target_pairs={{0,7},{1,0},{2,1},{3,2},{4,3},{5,4},{6,5},{7,6},{8,15},{9,8},{10,9... | collective-permute-start | bytes 1179656 | tf_op jit(solution)/shard_map/while/body/eval_jaxpr/ppermute | solution.py:107
  743.1 37.3 %collective-permute-start.1 = (bf16[256,768]{1,0:T(8,128)(2,1)}, bf16[256,768]{1,0:T(8,128)(2,1)S(1)}, u32[]{:S(2)}, u32[]{:S(2)}) collective-permute-start(bf16[256,768]{1,0:T(8,128)(2,1)} %get-tuple-element.1689), channel_id=1, source_target_pairs={{0,7},{1,0},{2,1},{3,2},{4,3},{5,4},{6,5},{7,6},{8,15},{9,8},{10,9... | collective-permute-start | bytes 1179656 | tf_op jit(solution)/shard_map/while/body/eval_jaxpr/ppermute | solution.py:107
  785.7 35.0 %conditional.5 = (bf16[256,768]{1,0:T(8,128)(2,1)}, f32[2,768,3072]{2,1,0:T(8,128)}, f32[2,3072,768]{2,1,0:T(8,128)}, bf16[8,256,768]{2,1,0:T(8,128)(2,1)}) conditional(s32[]{:T(128)} %convert_element_type.96, (f32[2,768,3072]{2,1,0:T(8,128)}, f32[2,3072,768]{2,1,0:T(8,128)}, bf16[8,256,768]{2,1,0:T(8,128)(2,1)}) %tuple.185, (s32[]{:T(128)}, ...), branch_computations={%region_6.6_spmd, %region_7.7_spmd.clone} | conditional | flops 4860346368 | bytes 130548376 | solution.py:106
  829.1 35.0 %conditional.5 = (bf16[256,768]{1,0:T(8,128)(2,1)}, f32[2,768,3072]{2,1,0:T(8,128)}, f32[2,3072,768]{2,1,0:T(8,128)}, bf16[8,256,768]{2,1,0:T(8,128)(2,1)}) conditional(s32[]{:T(128)} %convert_element_type.96, (f32[2,768,3072]{2,1,0:T(8,128)}, f32[2,3072,768]{2,1,0:T(8,128)}, bf16[8,256,768]{2,1,0:T(8,128)(2,1)}) %tuple.185, (s32[]{:T(128)}, ...), branch_computations={%region_6.6_spmd, %region_7.7_spmd.clone} | conditional | flops 4860346368 | bytes 130548376 | solution.py:106
  872.4 35.0 %conditional.5 = (bf16[256,768]{1,0:T(8,128)(2,1)}, f32[2,768,3072]{2,1,0:T(8,128)}, f32[2,3072,768]{2,1,0:T(8,128)}, bf16[8,256,768]{2,1,0:T(8,128)(2,1)}) conditional(s32[]{:T(128)} %convert_element_type.96, (f32[2,768,3072]{2,1,0:T(8,128)}, f32[2,3072,768]{2,1,0:T(8,128)}, bf16[8,256,768]{2,1,0:T(8,128)(2,1)}) %tuple.185, (s32[]{:T(128)}, ...), branch_computations={%region_6.6_spmd, %region_7.7_spmd.clone} | conditional | flops 4860346368 | bytes 130548376 | solution.py:106
  915.8 35.0 %conditional.5 = (bf16[256,768]{1,0:T(8,128)(2,1)}, f32[2,768,3072]{2,1,0:T(8,128)}, f32[2,3072,768]{2,1,0:T(8,128)}, bf16[8,256,768]{2,1,0:T(8,128)(2,1)}) conditional(s32[]{:T(128)} %convert_element_type.96, (f32[2,768,3072]{2,1,0:T(8,128)}, f32[2,3072,768]{2,1,0:T(8,128)}, bf16[8,256,768]{2,1,0:T(8,128)(2,1)}) %tuple.185, (s32[]{:T(128)}, ...), branch_computations={%region_6.6_spmd, %region_7.7_spmd.clone} | conditional | flops 4860346368 | bytes 130548376 | solution.py:106
  959.1 35.0 %conditional.5 = (bf16[256,768]{1,0:T(8,128)(2,1)}, f32[2,768,3072]{2,1,0:T(8,128)}, f32[2,3072,768]{2,1,0:T(8,128)}, bf16[8,256,768]{2,1,0:T(8,128)(2,1)}) conditional(s32[]{:T(128)} %convert_element_type.96, (f32[2,768,3072]{2,1,0:T(8,128)}, f32[2,3072,768]{2,1,0:T(8,128)}, bf16[8,256,768]{2,1,0:T(8,128)(2,1)}) %tuple.185, (s32[]{:T(128)}, ...), branch_computations={%region_6.6_spmd, %region_7.7_spmd.clone} | conditional | flops 4860346368 | bytes 130548376 | solution.py:106
  1002.4 35.0 %conditional.5 = (bf16[256,768]{1,0:T(8,128)(2,1)}, f32[2,768,3072]{2,1,0:T(8,128)}, f32[2,3072,768]{2,1,0:T(8,128)}, bf16[8,256,768]{2,1,0:T(8,128)(2,1)}) conditional(s32[]{:T(128)} %convert_element_type.96, (f32[2,768,3072]{2,1,0:T(8,128)}, f32[2,3072,768]{2,1,0:T(8,128)}, bf16[8,256,768]{2,1,0:T(8,128)(2,1)}) %tuple.185, (s32[]{:T(128)}, ...), branch_computations={%region_6.6_spmd, %region_7.7_spmd.clone} | conditional | flops 4860346368 | bytes 130548376 | solution.py:106
  1045.8 35.0 %conditional.5 = (bf16[256,768]{1,0:T(8,128)(2,1)}, f32[2,768,3072]{2,1,0:T(8,128)}, f32[2,3072,768]{2,1,0:T(8,128)}, bf16[8,256,768]{2,1,0:T(8,128)(2,1)}) conditional(s32[]{:T(128)} %convert_element_type.96, (f32[2,768,3072]{2,1,0:T(8,128)}, f32[2,3072,768]{2,1,0:T(8,128)}, bf16[8,256,768]{2,1,0:T(8,128)(2,1)}) %tuple.185, (s32[]{:T(128)}, ...), branch_computations={%region_6.6_spmd, %region_7.7_spmd.clone} | conditional | flops 4860346368 | bytes 130548376 | solution.py:106
  1089.1 35.0 %conditional.5 = (bf16[256,768]{1,0:T(8,128)(2,1)}, f32[2,768,3072]{2,1,0:T(8,128)}, f32[2,3072,768]{2,1,0:T(8,128)}, bf16[8,256,768]{2,1,0:T(8,128)(2,1)}) conditional(s32[]{:T(128)} %convert_element_type.96, (f32[2,768,3072]{2,1,0:T(8,128)}, f32[2,3072,768]{2,1,0:T(8,128)}, bf16[8,256,768]{2,1,0:T(8,128)(2,1)}) %tuple.185, (s32[]{:T(128)}, ...), branch_computations={%region_6.6_spmd, %region_7.7_spmd.clone} | conditional | flops 4860346368 | bytes 130548376 | solution.py:106
  1132.4 34.9 %conditional.5 = (bf16[256,768]{1,0:T(8,128)(2,1)}, f32[2,768,3072]{2,1,0:T(8,128)}, f32[2,3072,768]{2,1,0:T(8,128)}, bf16[8,256,768]{2,1,0:T(8,128)(2,1)}) conditional(s32[]{:T(128)} %convert_element_type.96, (f32[2,768,3072]{2,1,0:T(8,128)}, f32[2,3072,768]{2,1,0:T(8,128)}, bf16[8,256,768]{2,1,0:T(8,128)(2,1)}) %tuple.185, (s32[]{:T(128)}, ...), branch_computations={%region_6.6_spmd, %region_7.7_spmd.clone} | conditional | flops 4860346368 | bytes 130548376 | solution.py:106
  1175.8 34.9 %conditional.5 = (bf16[256,768]{1,0:T(8,128)(2,1)}, f32[2,768,3072]{2,1,0:T(8,128)}, f32[2,3072,768]{2,1,0:T(8,128)}, bf16[8,256,768]{2,1,0:T(8,128)(2,1)}) conditional(s32[]{:T(128)} %convert_element_type.96, (f32[2,768,3072]{2,1,0:T(8,128)}, f32[2,3072,768]{2,1,0:T(8,128)}, bf16[8,256,768]{2,1,0:T(8,128)(2,1)}) %tuple.185, (s32[]{:T(128)}, ...), branch_computations={%region_6.6_spmd, %region_7.7_spmd.clone} | conditional | flops 4860346368 | bytes 130548376 | solution.py:106
  1216.0 34.9 %conditional.5 = (bf16[256,768]{1,0:T(8,128)(2,1)}, f32[2,768,3072]{2,1,0:T(8,128)}, f32[2,3072,768]{2,1,0:T(8,128)}, bf16[8,256,768]{2,1,0:T(8,128)(2,1)}) conditional(s32[]{:T(128)} %convert_element_type.96, (f32[2,768,3072]{2,1,0:T(8,128)}, f32[2,3072,768]{2,1,0:T(8,128)}, bf16[8,256,768]{2,1,0:T(8,128)(2,1)}) %tuple.185, (s32[]{:T(128)}, ...), branch_computations={%region_6.6_spmd, %region_7.7_spmd.clone} | conditional | flops 4860346368 | bytes 130548376 | solution.py:106
  1256.2 34.9 %conditional.5 = (bf16[256,768]{1,0:T(8,128)(2,1)}, f32[2,768,3072]{2,1,0:T(8,128)}, f32[2,3072,768]{2,1,0:T(8,128)}, bf16[8,256,768]{2,1,0:T(8,128)(2,1)}) conditional(s32[]{:T(128)} %convert_element_type.96, (f32[2,768,3072]{2,1,0:T(8,128)}, f32[2,3072,768]{2,1,0:T(8,128)}, bf16[8,256,768]{2,1,0:T(8,128)(2,1)}) %tuple.185, (s32[]{:T(128)}, ...), branch_computations={%region_6.6_spmd, %region_7.7_spmd.clone} | conditional | flops 4860346368 | bytes 130548376 | solution.py:106
  1296.4 34.9 %conditional.5 = (bf16[256,768]{1,0:T(8,128)(2,1)}, f32[2,768,3072]{2,1,0:T(8,128)}, f32[2,3072,768]{2,1,0:T(8,128)}, bf16[8,256,768]{2,1,0:T(8,128)(2,1)}) conditional(s32[]{:T(128)} %convert_element_type.96, (f32[2,768,3072]{2,1,0:T(8,128)}, f32[2,3072,768]{2,1,0:T(8,128)}, bf16[8,256,768]{2,1,0:T(8,128)(2,1)}) %tuple.185, (s32[]{:T(128)}, ...), branch_computations={%region_6.6_spmd, %region_7.7_spmd.clone} | conditional | flops 4860346368 | bytes 130548376 | solution.py:106
  1336.6 34.9 %conditional.5 = (bf16[256,768]{1,0:T(8,128)(2,1)}, f32[2,768,3072]{2,1,0:T(8,128)}, f32[2,3072,768]{2,1,0:T(8,128)}, bf16[8,256,768]{2,1,0:T(8,128)(2,1)}) conditional(s32[]{:T(128)} %convert_element_type.96, (f32[2,768,3072]{2,1,0:T(8,128)}, f32[2,3072,768]{2,1,0:T(8,128)}, bf16[8,256,768]{2,1,0:T(8,128)(2,1)}) %tuple.185, (s32[]{:T(128)}, ...), branch_computations={%region_6.6_spmd, %region_7.7_spmd.clone} | conditional | flops 4860346368 | bytes 130548376 | solution.py:106
  1376.8 34.9 %conditional.5 = (bf16[256,768]{1,0:T(8,128)(2,1)}, f32[2,768,3072]{2,1,0:T(8,128)}, f32[2,3072,768]{2,1,0:T(8,128)}, bf16[8,256,768]{2,1,0:T(8,128)(2,1)}) conditional(s32[]{:T(128)} %convert_element_type.96, (f32[2,768,3072]{2,1,0:T(8,128)}, f32[2,3072,768]{2,1,0:T(8,128)}, bf16[8,256,768]{2,1,0:T(8,128)(2,1)}) %tuple.185, (s32[]{:T(128)}, ...), branch_computations={%region_6.6_spmd, %region_7.7_spmd.clone} | conditional | flops 4860346368 | bytes 130548376 | solution.py:106
  1417.2 34.9 %conditional.5 = (bf16[256,768]{1,0:T(8,128)(2,1)}, f32[2,768,3072]{2,1,0:T(8,128)}, f32[2,3072,768]{2,1,0:T(8,128)}, bf16[8,256,768]{2,1,0:T(8,128)(2,1)}) conditional(s32[]{:T(128)} %convert_element_type.96, (f32[2,768,3072]{2,1,0:T(8,128)}, f32[2,3072,768]{2,1,0:T(8,128)}, bf16[8,256,768]{2,1,0:T(8,128)(2,1)}) %tuple.185, (s32[]{:T(128)}, ...), branch_computations={%region_6.6_spmd, %region_7.7_spmd.clone} | conditional | flops 4860346368 | bytes 130548376 | solution.py:106
  1462.1 79.0 %all-reduce.7.cloned.1.call-done = (bf16[8,256,768]{2,1,0:T(8,128)(2,1)}, bf16[8,256,768]{2,1,0:T(8,128)(2,1)}) async-done(((bf16[8,256,768]{2,1,0:T(8,128)(2,1)}, bf16[8,256,768]{2,1,0:T(8,128)(2,1)}), (bf16[8,256,768]{2,1,0:T(8,128)(2,1)}, bf16[8,256,768]{2,1,0:T(8,128)(2,1)})) %all-reduce.7.cloned.1.call-update) | async-done | bytes 6291472 | tf_op jit(solution)/shard_map/psum | solution.py:111
  1541.0 631.0 %all-reduce.5.cloned.1.call-done = (f32[2,1,768,3072]{3,2,1,0:T(8,128)}, f32[2,1,3072,768]{3,2,1,0:T(8,128)}) async-done(((f32[2,1,768,3072]{3,2,1,0:T(8,128)}, f32[2,1,3072,768]{3,2,1,0:T(8,128)}), (f32[2,1,768,3072]{3,2,1,0:T(8,128)}, f32[2,1,3072,768]{3,2,1,0:T(8,128)})) %all-reduce.5.cloned.1.call-update) | async-done | bytes 37748752 | tf_op jit(solution)/shard_map/psum | solution.py:113
  2177.6 15.4 copy.66
  (569 shorter events, 1144.0 us)
Async XLA Ops:
  7.2 1533.8 %all-reduce.7.cloned.1.call-start = ((), (), s32[]{:S(2)}) async-start(), calls=%async_computation.1 | async-start | bytes 12582912 | tf_op jit(solution)/shard_map/psum | solution.py:111
  38.6 8.4 collective-permute-start
  58.5 8.4 collective-permute-start
  78.4 8.4 collective-permute-start
  98.2 8.4 collective-permute-start
  118.1 8.4 collective-permute-start
  138.0 8.4 collective-permute-start
  157.9 8.4 collective-permute-start
  177.8 8.4 collective-permute-start
  197.8 8.4 collective-permute-start
  217.8 8.4 collective-permute-start
  237.7 8.4 collective-permute-start
  257.8 8.4 collective-permute-start
  277.8 8.4 collective-permute-start
  297.8 8.4 collective-permute-start
  317.8 8.4 collective-permute-start
  337.8 8.4 collective-permute-start
  347.7 14.8 collective-permute-start
  364.0 14.8 collective-permute-start
  380.3 14.8 collective-permute-start
  396.6 14.7 collective-permute-start
  412.9 14.8 collective-permute-start
  429.2 15.9 collective-permute-start
  446.6 17.3 collective-permute-start
  486.6 38.7 %collective-permute-start.1 = (bf16[256,768]{1,0:T(8,128)(2,1)}, bf16[256,768]{1,0:T(8,128)(2,1)S(1)}, u32[]{:S(2)}, u32[]{:S(2)}) collective-permute-start(bf16[256,768]{1,0:T(8,128)(2,1)} %get-tuple-element.1689), channel_id=1, source_target_pairs={{0,7},{1,0},{2,1},{3,2},{4,3},{5,4},{6,5},{7,6},{8,15},{9,8},{10,9... | collective-permute-start | bytes 1179656 | tf_op jit(solution)/shard_map/while/body/eval_jaxpr/ppermute | solution.py:107
  526.1 42.6 %collective-permute-start.1 = (bf16[256,768]{1,0:T(8,128)(2,1)}, bf16[256,768]{1,0:T(8,128)(2,1)S(1)}, u32[]{:S(2)}, u32[]{:S(2)}) collective-permute-start(bf16[256,768]{1,0:T(8,128)(2,1)} %get-tuple-element.1689), channel_id=1, source_target_pairs={{0,7},{1,0},{2,1},{3,2},{4,3},{5,4},{6,5},{7,6},{8,15},{9,8},{10,9... | collective-permute-start | bytes 1179656 | tf_op jit(solution)/shard_map/while/body/eval_jaxpr/ppermute | solution.py:107
  569.5 42.6 %collective-permute-start.1 = (bf16[256,768]{1,0:T(8,128)(2,1)}, bf16[256,768]{1,0:T(8,128)(2,1)S(1)}, u32[]{:S(2)}, u32[]{:S(2)}) collective-permute-start(bf16[256,768]{1,0:T(8,128)(2,1)} %get-tuple-element.1689), channel_id=1, source_target_pairs={{0,7},{1,0},{2,1},{3,2},{4,3},{5,4},{6,5},{7,6},{8,15},{9,8},{10,9... | collective-permute-start | bytes 1179656 | tf_op jit(solution)/shard_map/while/body/eval_jaxpr/ppermute | solution.py:107
  612.9 42.6 %collective-permute-start.1 = (bf16[256,768]{1,0:T(8,128)(2,1)}, bf16[256,768]{1,0:T(8,128)(2,1)S(1)}, u32[]{:S(2)}, u32[]{:S(2)}) collective-permute-start(bf16[256,768]{1,0:T(8,128)(2,1)} %get-tuple-element.1689), channel_id=1, source_target_pairs={{0,7},{1,0},{2,1},{3,2},{4,3},{5,4},{6,5},{7,6},{8,15},{9,8},{10,9... | collective-permute-start | bytes 1179656 | tf_op jit(solution)/shard_map/while/body/eval_jaxpr/ppermute | solution.py:107
  656.3 42.6 %collective-permute-start.1 = (bf16[256,768]{1,0:T(8,128)(2,1)}, bf16[256,768]{1,0:T(8,128)(2,1)S(1)}, u32[]{:S(2)}, u32[]{:S(2)}) collective-permute-start(bf16[256,768]{1,0:T(8,128)(2,1)} %get-tuple-element.1689), channel_id=1, source_target_pairs={{0,7},{1,0},{2,1},{3,2},{4,3},{5,4},{6,5},{7,6},{8,15},{9,8},{10,9... | collective-permute-start | bytes 1179656 | tf_op jit(solution)/shard_map/while/body/eval_jaxpr/ppermute | solution.py:107
  699.7 42.6 %collective-permute-start.1 = (bf16[256,768]{1,0:T(8,128)(2,1)}, bf16[256,768]{1,0:T(8,128)(2,1)S(1)}, u32[]{:S(2)}, u32[]{:S(2)}) collective-permute-start(bf16[256,768]{1,0:T(8,128)(2,1)} %get-tuple-element.1689), channel_id=1, source_target_pairs={{0,7},{1,0},{2,1},{3,2},{4,3},{5,4},{6,5},{7,6},{8,15},{9,8},{10,9... | collective-permute-start | bytes 1179656 | tf_op jit(solution)/shard_map/while/body/eval_jaxpr/ppermute | solution.py:107
  743.1 42.6 %collective-permute-start.1 = (bf16[256,768]{1,0:T(8,128)(2,1)}, bf16[256,768]{1,0:T(8,128)(2,1)S(1)}, u32[]{:S(2)}, u32[]{:S(2)}) collective-permute-start(bf16[256,768]{1,0:T(8,128)(2,1)} %get-tuple-element.1689), channel_id=1, source_target_pairs={{0,7},{1,0},{2,1},{3,2},{4,3},{5,4},{6,5},{7,6},{8,15},{9,8},{10,9... | collective-permute-start | bytes 1179656 | tf_op jit(solution)/shard_map/while/body/eval_jaxpr/ppermute | solution.py:107
  820.7 8.4 collective-permute-start.1
  864.1 8.3 collective-permute-start.1
  907.4 8.3 collective-permute-start.1
  950.8 8.3 collective-permute-start.1
  994.1 8.3 collective-permute-start.1
  1037.4 8.3 collective-permute-start.1
  1080.8 8.3 collective-permute-start.1
  1124.1 8.3 collective-permute-start.1
  1167.4 8.4 collective-permute-start.1
  1210.7 5.3 collective-permute-start.1
  1250.9 5.3 collective-permute-start.1
  1291.1 5.3 collective-permute-start.1
  1331.3 5.3 collective-permute-start.1
  1371.5 5.3 collective-permute-start.1
  1411.7 5.6 collective-permute-start.1
  1452.1 5.3 collective-permute-start.1
  1461.2 710.8 %all-reduce.5.cloned.1.call-start = ((), (), s32[]{:S(2)}) async-start(), calls=%async_computation | async-start | bytes 75497472 | tf_op jit(solution)/shard_map/psum | solution.py:113
  (125 other events, 743.7 us)
Sparse Core Ops, SparseCore 0:
  1461.4 79.6 all-reduce.6
  1544.3 627.7 all-reduce.4
where the time goes:
time: 2210 us
  waiting for transfers between devices  1070 us (48%)
  matrix products  505 us (23%)
  starting transfers between devices  289 us (13%)
  local copies, waits for them, and re-layouts  272 us (12%)
  other arithmetic  56.2 us (3%)
    psum x1, waiting for transfers between devices, local_fn(): grad_first = lax.psum(acc_first, 'data')  631 us
    ppermute x23, starting transfers between devices, bwd_tick(): lax.ppermute(g_prev, 'stage', to_prev)  285 us
    ppermute x23, waiting for transfers between devices, fwd_tick(): return (lax.ppermute(h_out, 'stage', to_next), h_saved, pre_saved, y_buf)  238 us
    dynamic_slice x48, local copies, waits for them, and re-layouts, pick_row(): return lax.dynamic_index_in_dim(stacked, row_idx, 0, keepdims=False)  166 us
    dot_general x16, matrix products, layer_backward(): jnp.einsum('tf,td->fd', hidden, g_next, preferred_element_type=jnp.float32)  128 us
    ppermute x23, waiting for transfers between devices, bwd_tick(): lax.ppermute(g_prev, 'stage', to_prev)  122 us
    dot_general x16, matrix products, layer_backward(): jnp.einsum('td,fd->tf', g_next, w_second, preferred_element_type=jnp.floa...  108 us
    dot_general x16, matrix products, layer_backward(): jnp.einsum('td,tf->df', h_in, grad_pre, preferred_element_type=jnp.float32)  99.7 us
  transfers between devices with their start and end apart: 48, of which 48 were waited for; matrix products, arithmetic and copies ran while one was open for 0% of the time, Pallas kernels for 0%

commit v1 on v0

v1 whole, which is shorter than its diff:
```python
import functools
import jax
import jax.numpy as jnp
from jax import lax
from jax.experimental import pallas as pl
from jax.experimental.pallas import tpu as pltpu
from jax.sharding import PartitionSpec as P

MESH = pl.DeviceIdType.MESH
F32 = jnp.float32
BF16 = jnp.bfloat16
ANY = pl.BlockSpec(memory_space=pl.ANY)
GELU_A = 0.7978845608028654
GELU_B = 0.044715
VMEM_LIMIT = 66_000_000


def dot(a, b):
    return jnp.dot(a, b, preferred_element_type=F32)


def dot_tn(a, b):
    return lax.dot_general(a, b, (((0,), (0,)), ((), ())), preferred_element_type=F32)


def pick_block(size, target):
    block = min(size, target)
    while size % block:
        block //= 2
    return block


def stage_barrier(stages, levels, all_levels):
    s = lax.axis_index('stage')
    sem = pltpu.get_barrier_semaphore()
    count = 0
    for step in range(1, stages):
        pl.semaphore_signal(sem, inc=1, device_id={'stage': lax.rem(s + step, stages)}, device_id_type=MESH)
        count += 1
    if all_levels:
        d = lax.axis_index('data')
        for step in range(1, levels):
            pl.semaphore_signal(sem, inc=1, device_id={'data': lax.rem(d + step, levels)}, device_id_type=MESH)
            count += 1
    pl.semaphore_wait(sem, count)


def fwd_kernel(stages, levels, vees, micros, chunks, x_ref, wi_hbm, wo_hbm, *refs):
    h_outs, (y_out, wi, wo, hbuf, obuf, abuf, w_sem, x_sem, h_sem, y_sem, send_sem, recv_sem) = refs[:vees], refs[vees:]
    s = lax.axis_index('stage')
    nxt = lax.rem(s + 1, stages)
    _, dim, hid = wi.shape
    units = vees * micros
    fb = pick_block(hid, 512)
    nb = dim // chunks
    first = s == 0
    last = s == stages - 1

    def w_copies(v):
        return (pltpu.make_async_copy(wi_hbm.at[v], wi.at[v], w_sem.at[v, 0]),
                pltpu.make_async_copy(wo_hbm.at[v], wo.at[v], w_sem.at[v, 1]))

    def x_copy(m):
        return pltpu.make_async_copy(x_ref.at[m], hbuf.at[m], x_sem.at[m])

    def send(i, c, slot):
        cols = slice(c * nb, (c + 1) * nb)
        return pltpu.make_async_remote_copy(
            src_ref=obuf.at[i, :, cols], dst_ref=hbuf.at[slot, :, cols], send_sem=send_sem.at[i], recv_sem=recv_sem.at[slot],
            device_id={'stage': nxt}, device_id_type=MESH)

    def whole(i, slot):
        return pltpu.make_async_remote_copy(
            src_ref=obuf.at[i], dst_ref=hbuf.at[slot], send_sem=send_sem.at[i], recv_sem=recv_sem.at[slot],
            device_id={'stage': nxt}, device_id_type=MESH)

    def save(i, v):
        return pltpu.make_async_copy(hbuf.at[i], h_outs[v].at[i - v * micros], h_sem.at[i])

    for v in range(vees):
        for c in w_copies(v):
            c.start()

    @pl.when(first)
    def _():
        lax.fori_loop(0, micros, lambda m, _: (x_copy(m).start(), 0)[1], 0)

    stage_barrier(stages, levels, False)

    def unit(i, v):
        slot = jnp.where(last, i + micros, i)
        local_in = first & (v == 0)
        final = last & (v == vees - 1)

        @pl.when(local_in)
        def _():
            x_copy(i).wait()

        @pl.when(jnp.logical_not(local_in))
        def _():
            whole(i, i).wait_recv()

        save(i, v).start()
        for f in range(hid // fb):
            cols = slice(f * fb, (f + 1) * fb)
            z = dot(hbuf[i], wi[v, :, cols])
            t = jnp.tanh(GELU_A * (z + GELU_B * (z * z * z)))
            abuf[:, cols] = (z * (0.5 * (1.0 + t))).astype(BF16)
        for c in range(chunks):
            cols = slice(c * nb, (c + 1) * nb)
            out = hbuf[i, :, cols].astype(F32) + dot(abuf[...], wo[v, :, cols])
            obuf[i, :, cols] = out.astype(BF16)

            @pl.when(jnp.logical_not(final))
            def _():
                send(i, c, slot).start()

        @pl.when(final)
        def _():
            pltpu.make_async_copy(obuf.at[i], y_out.at[i - (vees - 1) * micros], y_sem.at[i - (vees - 1) * micros]).start()

    for v in range(vees):
        for c in w_copies(v):
            c.wait()

        def body(m, _, v=v):
            unit(v * micros + m, v)
            return 0
        lax.fori_loop(0, micros, body, 0)

    def drain(i, v):
        save(i, v).wait()
        final = last & (v == vees - 1)

        @pl.when(jnp.logical_not(final))
        def _():
            whole(i, i).wait_send()

        @pl.when(final)
        def _():
            pltpu.make_async_copy(obuf.at[i], y_out.at[i - (vees - 1) * micros], y_sem.at[i - (vees - 1) * micros]).wait()

    for v in range(vees):
        def tail(m, _, v=v):
            drain(v * micros + m, v)
            return 0
        lax.fori_loop(0, micros, tail, 0)


def run_fwd(stages, levels, x, w_in, w_out):
    micros, tokens, dim = x.shape
    vees, _, hid = w_in.shape
    units = vees * micros
    chunks = 3 if dim % 384 == 0 else 1
    flops = units * 4 * tokens * dim * hid
    return pl.pallas_call(
        functools.partial(fwd_kernel, stages, levels, vees, micros, chunks),
        out_shape=(jax.ShapeDtypeStruct((micros, tokens, dim), BF16),) * (vees + 1),
        in_specs=[ANY] * 3, out_specs=(ANY,) * (vees + 1),
        scratch_shapes=[
            pltpu.VMEM((vees, dim, hid), BF16), pltpu.VMEM((vees, hid, dim), BF16),
            pltpu.VMEM((units, tokens, dim), BF16), pltpu.VMEM((units, tokens, dim), BF16), pltpu.VMEM((tokens, hid), BF16),
            pltpu.SemaphoreType.DMA((vees, 2)), pltpu.SemaphoreType.DMA((micros,)), pltpu.SemaphoreType.DMA((units,)),
            pltpu.SemaphoreType.DMA((micros,)), pltpu.SemaphoreType.DMA((units,)), pltpu.SemaphoreType.DMA((units,)),
        ],
        compiler_params=pltpu.CompilerParams(collective_id=0, has_side_effects=True, vmem_limit_bytes=VMEM_LIMIT),
        cost_estimate=pl.CostEstimate(flops=flops, bytes_accessed=2 * units * tokens * dim * 2, transcendentals=units * tokens * hid),
        name='fwd_pipe',
    )(x, w_in, w_out)


def bwd_kernel(stages, levels, micros, groups, chunks, v, *refs):
    wide = groups > 1
    if wide:
        (h_hbm, e_hbm, _, wi_hbm, wo_hbm, gin_hbm, gout_hbm, dx_out, y_out, wi, wit, wot, tmp, gin, gout, ebuf, hbuf, obuf, abuf, qbuf,
         w_sem, t_sem, h_sem, l_sem, g_sem, send_sem, recv_sem, relay_send, dx_sem, dx_send, dx_recv, y_send, y_recv) = refs
    else:
        (h_hbm, e_hbm, wi_hbm, wo_hbm, gin_hbm, gout_hbm, dx_out, wi, wit, wot, tmp, gin, gout, ebuf, hbuf, obuf, abuf, qbuf,
         w_sem, t_sem, h_sem, l_sem, g_sem, send_sem, recv_sem, dx_sem) = refs
    s = lax.axis_index('stage')
    d = lax.axis_index('data')
    prv = lax.rem(s + stages - 1, stages)
    dim, hid = wi.shape
    units = groups * micros
    fb = pick_block(hid, 512)
    nb = dim // chunks
    tb = tmp.shape[1]
    hslots = hbuf.shape[0]
    oslots = obuf.shape[0]
    first = s == 0
    last = s == stages - 1

    def row_of(i):
        if not wide:
            return i
        return lax.rem(d + i // micros, levels) * micros + lax.rem(i, micros)

    def h_copy(i):
        return pltpu.make_async_copy(h_hbm.at[row_of(i)], hbuf.at[lax.rem(i, hslots)], h_sem.at[lax.rem(i, hslots)])

    def e_copy(m):
        return pltpu.make_async_copy(e_hbm.at[m], ebuf.at[m], l_sem.at[m])

    def hop(i, c=None):
        o = lax.rem(i, oslots)
        if c is None:
            src, dst = obuf.at[o], ebuf.at[i]
        else:
            cols = slice(c * nb, (c + 1) * nb)
            src, dst = obuf.at[o, :, cols], ebuf.at[i, :, cols]
        return pltpu.make_async_remote_copy(src_ref=src, dst_ref=dst, send_sem=send_sem.at[o], recv_sem=recv_sem.at[i],
                                            device_id={'stage': prv}, device_id_type=MESH)

    def entry(m):
        return pltpu.make_async_remote_copy(src_ref=e_hbm.at[m], dst_ref=ebuf.at[m], send_sem=l_sem.at[m], recv_sem=recv_sem.at[m],
                                            device_id={'stage': prv}, device_id_type=MESH)

    def dx_copy(m):
        return pltpu.make_async_copy(obuf.at[m], dx_out.at[m], dx_sem.at[m])

    def relay(m, j):
        slot = (levels - j) * micros + m
        return pltpu.make_async_remote_copy(src_ref=ebuf.at[m], dst_ref=ebuf.at[slot], send_sem=relay_send.at[m, j - 1],
                                            recv_sem=recv_sem.at[slot], device_id={'data': lax.rem(d + j, levels)}, device_id_type=MESH)

    def share(src, dst, send, recv, m, j):
        return pltpu.make_async_remote_copy(src_ref=src.at[m], dst_ref=dst.at[m], send_sem=send.at[m, j - 1], recv_sem=recv.at[m],
                                            device_id={'stage': lax.rem(s + j, stages)}, device_id_type=MESH)

    def loop(lo, hi, fn):
        def body(i, _):
            fn(i)
            return 0
        lax.fori_loop(lo, hi, body, 0)

    wi_copy = pltpu.make_async_copy(wi_hbm.at[v], wi, w_sem)
    wi_copy.start()

    def wo_copy(b):
        return pltpu.make_async_copy(wo_hbm.at[v, pl.ds(b * tb, tb)], tmp.at[b % 2], t_sem.at[b % 2])

    wo_copy(0).start()
    h_copy(0).start()
    gin[...] = jnp.zeros_like(gin)
    gout[...] = jnp.zeros_like(gout)
    wi_copy.wait()
    for b in range(hid // tb):
        rows = slice(b * tb, (b + 1) * tb)
        if b + 1 < hid // tb:
            wo_copy(b + 1).start()
        wit[rows, :] = wi[:, rows].T
        wo_copy(b).wait()
        wot[:, rows] = tmp[b % 2].T

    stage_barrier(stages, levels, wide)

    if wide:
        @pl.when(first)
        def _():
            loop(0, micros, lambda m: entry(m).start())
    else:
        @pl.when(last)
        def _():
            loop(0, micros, lambda m: e_copy(m).start())

    def unit(i):
        hs = lax.rem(i, hslots)
        o = lax.rem(i, oslots)
        h_copy(i).wait()

        @pl.when(i + 1 < units)
        def _():
            h_copy(i + 1).start()

        if wide:
            hop(i).wait_recv()

            @pl.when(last & (i < micros))
            def _():
                for j in range(1, levels):
                    relay(i, j).start()

            @pl.when(last & (i >= micros) & (i < 2 * micros))
            def _():
                m = i - micros
                for j in range(1, stages):
                    share(y_out, y_out, y_send, y_recv, m, j).start()
        else:
            @pl.when(last)
            def _():
                e_copy(i).wait()

            @pl.when(jnp.logical_not(last))
            def _():
                hop(i).wait_recv()

        for f in range(hid // fb):
            cols = slice(f * fb, (f + 1) * fb)
            z = dot(hbuf[hs], wi[:, cols])
            ga = dot(ebuf[i], wot[:, cols])
            z2 = z * z
            t = jnp.tanh(GELU_A * (z + GELU_B * (z2 * z)))
            cdf = 0.5 * (1.0 + t)
            slope = cdf + (0.5 * z) * (1.0 - t * t) * (GELU_A * (1.0 + (3.0 * GELU_B) * z2))
            abuf[:, cols] = (z * cdf).astype(BF16)
            qbuf[:, cols] = (slope * ga).astype(BF16)

        @pl.when(jnp.logical_not(first) & (i >= oslots))
        def _():
            hop(i - oslots).wait_send()

        @pl.when(jnp.logical_not(first) | (i < micros))
        def _():
            for c in range(chunks):
                cols = slice(c * nb, (c + 1) * nb)
                out = ebuf[i, :, cols].astype(F32) + dot(qbuf[...], wit[:, cols])
                obuf[o, :, cols] = out.astype(BF16)

                @pl.when(jnp.logical_not(first))
                def _():
                    hop(i, c).start()

        @pl.when(first & (i < micros))
        def _():
            dx_copy(i).start()
            if wide:
                for j in range(1, stages):
                    share(obuf, dx_out, dx_send, dx_recv, i, j).start()

        for f in range(hid // fb):
            cols = slice(f * fb, (f + 1) * fb)
            gin[:, cols] += dot_tn(hbuf[hs], qbuf[:, cols])
            gout[cols, :] += dot_tn(abuf[:, cols], ebuf[i])

    loop(0, units, unit)

    gin_copy = pltpu.make_async_copy(gin, gin_hbm, g_sem.at[0])
    gout_copy = pltpu.make_async_copy(gout, gout_hbm, g_sem.at[1])
    gin_copy.start()
    gout_copy.start()

    @pl.when(jnp.logical_not(first))
    def _():
        loop(units - oslots, units, lambda i: hop(i).wait_send())

    @pl.when(first)
    def _():
        loop(0, micros, lambda m: dx_copy(m).wait())

    if wide:
        @pl.when(first)
        def _():
            loop(0, micros, lambda m: entry(m).wait_send())
            for j in range(1, stages):
                loop(0, micros, lambda m, j=j: share(obuf, dx_out, dx_send, dx_recv, m, j).wait_send())

        @pl.when(last)
        def _():
            for j in range(1, levels):
                loop(0, micros, lambda m, j=j: relay(m, j).wait_send())
            for j in range(1, stages):
                loop(0, micros, lambda m, j=j: share(y_out, y_out, y_send, y_recv, m, j).wait_send())

        @pl.when(jnp.logical_not(first))
        def _():
            loop(0, micros, lambda m: share(obuf, dx_out, dx_send, dx_recv, m, 1).wait_recv())

        @pl.when(jnp.logical_not(last))
        def _():
            loop(0, micros, lambda m: share(y_out, y_out, y_send, y_recv, m, 1).wait_recv())

    gin_copy.wait()
    gout_copy.wait()


def run_bwd(stages, levels, v, h, e, y, wi, wo):
    micros, tokens, dim = e.shape
    hid = wi.shape[2]
    wide = y is not None
    groups = h.shape[0] // micros
    units = groups * micros
    chunks = 3 if dim % 384 == 0 else 1
    tb = pick_block(hid, 768)
    dma = pltpu.SemaphoreType.DMA
    small = jax.ShapeDtypeStruct((micros, tokens, dim), BF16)
    out_shape = [jax.ShapeDtypeStruct((dim, hid), F32), jax.ShapeDtypeStruct((hid, dim), F32), small]
    operands = [h, e]
    scratch = [
        pltpu.VMEM((dim, hid), BF16), pltpu.VMEM((hid, dim), BF16), pltpu.VMEM((dim, hid), BF16), pltpu.VMEM((2, tb, dim), BF16),
        pltpu.VMEM((dim, hid), F32), pltpu.VMEM((hid, dim), F32), pltpu.VMEM((units, tokens, dim), BF16),
        pltpu.VMEM((2, tokens, dim), BF16), pltpu.VMEM((micros, tokens, dim), BF16),
        pltpu.VMEM((tokens, hid), BF16), pltpu.VMEM((tokens, hid), BF16),
        dma, dma((2,)), dma((2,)), dma((micros,)), dma((2,)), dma((micros,)), dma((units,)),
    ]
    aliases = {}
    if wide:
        operands.append(y)
        out_shape.append(small)
        aliases = {2: 3}
        scratch += [dma((micros, levels - 1)), dma((micros,)), dma((micros, stages - 1)), dma((micros,)),
                    dma((micros, stages - 1)), dma((micros,))]
    else:
        scratch += [dma((micros,))]
    operands += [wi, wo]
    return pl.pallas_call(
        functools.partial(bwd_kernel, stages, levels, micros, groups, chunks, v),
        out_shape=tuple(out_shape), in_specs=[ANY] * len(operands), out_specs=(ANY,) * len(out_shape),
        scratch_shapes=scratch, input_output_aliases=aliases,
        compiler_params=pltpu.CompilerParams(collective_id=2 if wide else 1, has_side_effects=True, vmem_limit_bytes=VMEM_LIMIT),
        cost_estimate=pl.CostEstimate(flops=units * 10 * tokens * dim * hid, bytes_accessed=units * tokens * dim * 4,
                                      transcendentals=units * tokens * hid),
        name='bwd_wide' if wide else 'bwd_own',
    )(*operands)


def solution(mesh):
    stages, levels = mesh.shape['stage'], mesh.shape['data']

    def local_fn(x, g, w_in, w_out):
        wi, wo = w_in[:, 0], w_out[:, 0]
        h_lo, h_up, y = run_fwd(stages, levels, x, wi, wo)
        h_all = lax.all_gather(h_lo, 'data', axis=0, tiled=True)
        gin_up, gout_up, e_mid = run_bwd(stages, levels, 1, h_up, g, None, wi, wo)
        gin_up, gout_up = lax.psum((gin_up, gout_up), 'data')
        gin_lo, gout_lo, dx, y = run_bwd(stages, levels, 0, h_all, e_mid, y, wi, wo)
        grad_in = jnp.stack([gin_lo, gin_up])[:, None]
        grad_out = jnp.stack([gout_lo, gout_up])[:, None]
        return y, dx, grad_in, grad_out

    spec_rows = P(('part', 'data'))
    spec_weights = P(None, 'stage')
    spec_grads = P('part', 'stage')
    return jax.shard_map(local_fn, mesh=mesh, in_specs=(spec_rows, spec_rows, spec_weights, spec_weights), out_specs=(spec_rows, spec_rows, spec_grads, spec_grads), check_vma=False)
```

time: 2210 us -> 776 us (0.35)
  waiting for transfers between devices: 1070 us -> 0.15 us
  Pallas kernels: 0 us -> 731 us
  matrix products: 505 us -> 0 us
  starting transfers between devices: 289 us -> 0.13 us
  local copies, waits for them, and re-layouts: 272 us -> 6.82 us
  other arithmetic: 56.2 us -> 23 us
    pallas_call x0 -> x3, Pallas kernels: none -> 731 us  [the longest x2 633 us: run_bwd(): pl.pallas_call(functools.partial(bwd_kernel, stages, levels, micros, grou...]
    psum x2 -> x1, waiting for transfers between devices: 710 us -> 0.02 us  [local_fn(): gin_up, gout_up = lax.psum((gin_up, gout_up), 'data')]
    dot_general x96 -> x0, matrix products: 505 us -> none  [the longest x16 128 us: layer_backward(): jnp.einsum('tf,td->fd', hidden, g_next, preferred_element_type=jnp.float32)]
    ppermute x46 -> x0, waiting for transfers between devices: 360 us -> none  [the longest x23 238 us: fwd_tick(): return (lax.ppermute(h_out, 'stage', to_next), h_saved, pre_saved, y_buf)]
    ppermute x46 -> x0, starting transfers between devices: 289 us -> none  [the longest x23 285 us: bwd_tick(): lax.ppermute(g_prev, 'stage', to_prev)]
    dynamic_slice x48 -> x0, local copies, waits for them, and re-layouts: 166 us -> none  [pick_row(): return lax.dynamic_index_in_dim(stacked, row_idx, 0, keepdims=False)]
    broadcast_in_dim x4 -> x0, local copies, waits for them, and re-layouts: 36.8 us -> none  [the longest x1 16.3 us: local_fn(): jnp.zeros((unit_count, tokens, hidden_dim), jnp.float32)]
    dynamic_update_slice x16 -> x0, other arithmetic: 32.5 us -> none  [put_row(): return lax.dynamic_update_index_in_dim(stacked, row_val, row_idx, 0)]
  transfers between devices with their start and end apart: 48 -> 2, of which waited for: 48 -> 0; matrix products, arithmetic and copies ran while one was open for 0% -> 0% of each run, Pallas kernels for 0% -> 82%
where the time goes in v1:
time: 776 us
  Pallas kernels  731 us (94%)
  other arithmetic  23 us (3%)
  between operations  14.1 us (2%)
    pallas_call x2, Pallas kernels, run_bwd(): pl.pallas_call(functools.partial(bwd_kernel, stages, levels, micros, grou...  633 us
    pallas_call x1, Pallas kernels, run_fwd(): pl.pallas_call(functools.partial(fwd_kernel, stages, levels, vees, micros...  98.6 us
    unnamed x2, other arithmetic  23 us
  transfers between devices with their start and end apart: 2, of which 0 were waited for; matrix products, arithmetic and copies ran while one was open for 0% of the time, Pallas kernels for 82%

profile of v1, /device:TPU:96, one launch (start us, length us, event | category | flops | bytes accessed | tf_op | source)
XLA Modules:
  0.0 775.7 jit_solution(17539253502960970779)
XLA Ops:
  7.2 0.1 all-gather.2.cloned.1.call-start
  7.2 98.6 %fwd_pipe.1 = (bf16[8,256,768]{2,1,0:T(8,128)(2,1)}, bf16[8,256,768]{2,1,0:T(8,128)(2,1)}, bf16[8,256,768]{2,1,0:T(8,128)(2,1)}) custom-call(bf16[8,256,768]{2,1,0:T(8,128)(2,1)} %x_ref.1, bf16[2,768,3072]{2,1,0:T(8,128)(2,1)} %bitcast.18, bf16[2,3072,768]{2,1,0:T(8,128)(2,1)} %bitcast.21), custom_call_target="tpu_custom_call" | custom-call | flops 38654705664 | bytes 12582912 | tf_op jit(solution)/shard_map/fwd_pipe/pallas_call | solution.py:156
  105.8 0.1 all-gather.2.cloned.1.call-update
  105.9 0.1 all-reduce.3.cloned.1.call-start
  106.0 195.3 %bwd_own.1 = (f32[768,3072]{1,0:T(8,128)}, f32[3072,768]{1,0:T(8,128)}, bf16[8,256,768]{2,1,0:T(8,128)(2,1)}) custom-call(bf16[8,256,768]{2,1,0:T(8,128)(2,1)} %get-tuple-element.15.refs_0_, bf16[8,256,768]{2,1,0:T(8,128)(2,1)} %refs_1_.1, bf16[2,768,3072]{2,1,0:T(8,128)(2,1)} %bitcast.19, bf16[2,3072,768]{2,1,0:T(8,128)(2,1)} %bitcast.22), custom_call_target="tpu_custom_call" | custom-call | flops 48318382080 | bytes 6291456 | tf_op jit(solution)/shard_map/bwd_own/pallas_call | solution.py:405
  301.3 0.1 all-reduce.3.cloned.1.call-update
  301.4 0.0 all-gather.2.cloned.1.call-done.refs_0_
  301.4 437.6 %bwd_wide.1 = (f32[768,3072]{1,0:T(8,128)}, f32[3072,768]{1,0:T(8,128)}, bf16[8,256,768]{2,1,0:T(8,128)(2,1)}, bf16[8,256,768]{2,1,0:T(8,128)(2,1)}) custom-call(bf16[32,256,768]{2,1,0:T(8,128)(2,1)} %all-gather.2.cloned.1.call-done.refs_0_, bf16[8,256,768]{2,1,0:T(8,128)(2,1)} %get-tuple-element.16.refs_1_, ...), custom_call_target="tpu_custom_call", output_to_operand_aliasing={{3}: (2, {})} | custom-call | flops 193273528320 | bytes 25165824 | tf_op jit(solution)/shard_map/bwd_wide/pallas_call | solution.py:405
  739.0 0.0 all-reduce.3.cloned.1.call-done
  739.0 0.0 copy-start
  739.0 0.0 copy-start.1
  739.0 14.9 %maximum_bitcast_fusion = f32[2,1,768,3072]{3,2,1,0:T(8,128)} fusion(f32[1,768,3072]{2,1,0:T(8,128)} %get-tuple-element.32, f32[1,768,3072]{2,1,0:T(8,128)} %bitcast.17), kind=kLoop, calls=%fused_computation | loop fusion | flops 4718592 | bytes 37748736
  753.9 0.3 copy-done
  754.2 3.2 copy-done.1
  757.4 0.0 copy-start.2
  757.4 0.0 copy-start.3
  757.4 8.1 %maximum_bitcast_fusion.1 = f32[2,1,3072,768]{3,2,1,0:T(8,128)} fusion(f32[1,3072,768]{2,1,0:T(8,128)S(1)} %copy-done, f32[1,3072,768]{2,1,0:T(8,128)S(1)} %bitcast.16), kind=kLoop, calls=%fused_computation.1 | loop fusion | flops 4718592 | bytes 37748736
  765.5 0.0 copy-done.2
  765.5 1.7 copy.18
  767.1 0.0 copy-done.3
  767.1 1.7 copy.19
Async XLA Ops:
  7.2 294.2 %all-gather.2.cloned.1.call-start = ((), (), s32[]{:S(2)}) async-start(), calls=%async_computation | async-start | bytes 15728640 | tf_op jit(solution)/shard_map/all_gather | solution.py:422
  105.9 633.1 %all-reduce.3.cloned.1.call-start = ((), (), s32[]{:S(2)}) async-start(), calls=%async_computation.1 | async-start | bytes 37748736 | tf_op jit(solution)/shard_map/psum | solution.py:424
  739.0 15.2 %copy-start = (f32[1,3072,768]{2,1,0:T(8,128)S(1)}, f32[1,3072,768]{2,1,0:T(8,128)}, u32[]{:S(2)}) copy-start(f32[1,3072,768]{2,1,0:T(8,128)} %get-tuple-element.33) | copy-start | bytes 28311556
  739.0 18.3 %copy-start.1 = (f32[3072,768]{1,0:T(8,128)S(1)}, f32[3072,768]{1,0:T(8,128)}, u32[]{:S(2)}) copy-start(f32[3072,768]{1,0:T(8,128)} %get-tuple-element.22) | copy-start | bytes 28311556
  757.4 8.1 %copy-start.2 = (bf16[8,256,768]{2,1,0:T(8,128)(2,1)S(1)}, bf16[8,256,768]{2,1,0:T(8,128)(2,1)}, u32[]{:S(2)}) copy-start(bf16[8,256,768]{2,1,0:T(8,128)(2,1)} %get-tuple-element.38) | copy-start | bytes 9437188
  757.4 9.8 %copy-start.3 = (bf16[8,256,768]{2,1,0:T(8,128)(2,1)S(1)}, bf16[8,256,768]{2,1,0:T(8,128)(2,1)}, u32[]{:S(2)}) copy-start(bf16[8,256,768]{2,1,0:T(8,128)(2,1)} %get-tuple-element.39) | copy-start | bytes 9437188
Sparse Core Ops, SparseCore 0:
  106.0 164.3 all-gather.1
  301.5 390.7 all-reduce.2

commit v2 on v0

v2 whole, which is shorter than its diff:
```python
import functools
import jax
import jax.numpy as jnp
from jax import lax
from jax.experimental import pallas as pl
from jax.experimental.pallas import tpu as pltpu
from jax.sharding import PartitionSpec as P

MESH = pl.DeviceIdType.MESH
F32 = jnp.float32
BF16 = jnp.bfloat16
ANY = pl.BlockSpec(memory_space=pl.ANY)
GELU_A = 0.7978845608028654
GELU_B = 0.044715
VMEM_LIMIT = 66_000_000


def dot(a, b):
    return jnp.dot(a, b, preferred_element_type=F32)


def dot_nt(a, b):
    return lax.dot_general(a, b, (((1,), (1,)), ((), ())), preferred_element_type=F32)


def dot_tn(a, b):
    return lax.dot_general(a, b, (((0,), (0,)), ((), ())), preferred_element_type=F32)


def gelu_only(z):
    t = jnp.tanh(z * (GELU_A + (GELU_A * GELU_B) * (z * z)))
    return z * (0.5 * t + 0.5)


def gelu_and_slope(z):
    s = (GELU_A * GELU_B) * (z * z)
    cdf = 0.5 * jnp.tanh(z * (GELU_A + s)) + 0.5
    a = z * cdf
    return a, cdf + (a * (1.0 - cdf)) * (2.0 * GELU_A + 6.0 * s)


def pick_block(size, target):
    block = min(size, target)
    while size % block:
        block //= 2
    return block


def loop(lo, hi, fn):
    def body(i, _):
        fn(i)
        return 0
    lax.fori_loop(lo, hi, body, 0)


def signal_all(targets):
    sem = pltpu.get_barrier_semaphore()
    for target in targets:
        pl.semaphore_signal(sem, inc=1, device_id=target, device_id_type=MESH)
    pl.semaphore_wait(sem, len(targets))


def slices(size, block):
    return [slice(b * block, (b + 1) * block) for b in range(size // block)]


def act_pass(h, wi, a, slope, fb):
    for cols in slices(wi.shape[1], fb):
        act, der = gelu_and_slope(dot(h[...], wi[:, cols]))
        a[:, cols] = act.astype(BF16)
        slope[:, cols] = der


def grad_pass(h, e, q, a, gin, gout, h_next, wi, a_next, slope, fb):
    for cols in slices(wi.shape[1], fb):
        gin[:, cols] += dot_tn(h[...], q[:, cols])
        gout[cols, :] += dot_tn(a[:, cols], e[...])
        act, der = gelu_and_slope(dot(h_next[...], wi[:, cols]))
        a_next[:, cols] = act.astype(BF16)
        slope[:, cols] = der


def front_kernel(stages, levels, micros, chunks, x_hbm, g_hbm, wi_hbm, wo_hbm, hall, y_out, eall, gin_hbm, gout_hbm,
                 wi, wo, hbuf, obuf, ebuf, gin, gout, abuf, qbuf, slope,
                 w_sem, x_sem, g_sem, f_send, f_recv, b_send, b_recv, y_sem, h_save, h_send, h_recv, e_save, e_send, e_recv, o_sem):
    s = lax.axis_index('stage')
    d = lax.axis_index('data')
    nxt, prv = lax.rem(s + 1, stages), lax.rem(s + stages - 1, stages)
    up, down = lax.rem(d + 1, levels), lax.rem(d + levels - 1, levels)
    _, dim, hid = wi.shape
    tokens = hbuf.shape[1]
    half = tokens // 2
    nb = dim // chunks
    fb = pick_block(hid, 768)
    first = s == 0
    last = s == stages - 1
    lag = jnp.minimum(3 * (stages - 1 - s) + 1, micros)

    def w_copies(v):
        return (pltpu.make_async_copy(wi_hbm.at[v], wi.at[v], w_sem.at[v, 0]),
                pltpu.make_async_copy(wo_hbm.at[v], wo.at[v], w_sem.at[v, 1]))

    def x_copy(m):
        return pltpu.make_async_copy(x_hbm.at[m], hbuf.at[m], x_sem.at[m])

    def g_copy(m):
        return pltpu.make_async_copy(g_hbm.at[m], ebuf.at[m], g_sem.at[m])

    def f_hop(i, slot, cols=slice(None)):
        return pltpu.make_async_remote_copy(
            src_ref=obuf.at[lax.rem(i, micros), :, cols], dst_ref=hbuf.at[slot, :, cols], send_sem=f_send.at[i], recv_sem=f_recv.at[slot],
            device_id={'stage': nxt}, device_id_type=MESH)

    def b_hop(m, cols=slice(None)):
        return pltpu.make_async_remote_copy(
            src_ref=obuf.at[m, :, cols], dst_ref=ebuf.at[m, :, cols], send_sem=b_send.at[m], recv_sem=b_recv.at[m],
            device_id={'stage': prv}, device_id_type=MESH)

    def y_copy(m):
        return pltpu.make_async_copy(obuf.at[m], y_out.at[m], y_sem.at[m])

    def h_keep(m):
        return pltpu.make_async_copy(hbuf.at[m], hall.at[m], h_save.at[m])

    def h_push(m, j):
        return pltpu.make_async_remote_copy(
            src_ref=hbuf.at[m], dst_ref=hall.at[(2 - j) * micros + m], send_sem=h_send.at[j, m], recv_sem=h_recv.at[1 - j, m],
            device_id={'data': (up, down)[j]}, device_id_type=MESH)

    def h_forward(m, j):
        rows = (slice(0, half), slice(half, tokens))[j]
        return pltpu.make_async_remote_copy(
            src_ref=hall.at[(2 - j) * micros + m, rows], dst_ref=hall.at[3 * micros + m, rows], send_sem=h_send.at[2 + j, m],
            recv_sem=h_recv.at[2, m], device_id={'data': (up, down)[j]}, device_id_type=MESH)

    def h_whole(m):
        return pltpu.make_async_remote_copy(
            src_ref=hall.at[m], dst_ref=hall.at[3 * micros + m], send_sem=h_send.at[2, m], recv_sem=h_recv.at[2, m],
            device_id={'data': up}, device_id_type=MESH)

    def e_keep(m):
        return pltpu.make_async_copy(obuf.at[m], eall.at[m], e_save.at[m])

    def e_push(m, j):
        return pltpu.make_async_remote_copy(
            src_ref=obuf.at[m], dst_ref=eall.at[(2 - j) * micros + m], send_sem=e_send.at[j, m], recv_sem=e_recv.at[1 - j, m],
            device_id={'data': (up, down)[j]}, device_id_type=MESH)

    for v in range(2):
        for c in w_copies(v):
            c.start()

    @pl.when(first)
    def _():
        loop(0, micros, lambda m: x_copy(m).start())

    @pl.when(last)
    def _():
        loop(0, micros, lambda m: g_copy(m).start())

    signal_all([{'stage': lax.rem(s + step, stages)} for step in range(1, stages)] + [{'data': up}, {'data': down}])

    for c in w_copies(0):
        c.wait()

    def fwd_unit(i, a):
        v = i // micros
        lower = i < micros
        o = lax.rem(i, micros)
        slot = jnp.where(last, i + micros, i)
        final = last & jnp.logical_not(lower)

        @pl.when(first & lower)
        def _():
            x_copy(i).wait()

        @pl.when(jnp.logical_not(first & lower))
        def _():
            f_hop(i, i).wait_recv()

        @pl.when(lower)
        def _():
            h_keep(i).start()
            h_push(i, 0).start()
            h_push(i, 1).start()

        @pl.when(jnp.logical_not(lower))
        def _():
            f_hop(o, o).wait_send()
            h_push(o, 0).wait_recv()
            h_push(o, 1).wait_recv()
            h_forward(o, 0).start()
            h_forward(o, 1).start()

        for cols in slices(hid, fb):
            a[:, cols] = gelu_only(dot(hbuf[i], wi[v, :, cols])).astype(BF16)
        for cols in slices(dim, nb):
            out = hbuf[i, :, cols].astype(F32) + dot(a[...], wo[v, :, cols])
            obuf[o, :, cols] = out.astype(BF16)

            @pl.when(jnp.logical_not(final))
            def _():
                f_hop(i, slot, cols).start()

        @pl.when(final)
        def _():
            y_copy(o).start()

    def bwd_unit(m):
        a, a_next = abuf.at[lax.rem(m, 2)], abuf.at[lax.rem(m + 1, 2)]
        h, h_next = hbuf.at[micros + m], hbuf.at[micros + jnp.minimum(m + 1, micros - 1)]

        @pl.when(last)
        def _():
            g_copy(m).wait()
            y_copy(m).wait()

        @pl.when(jnp.logical_not(last))
        def _():
            b_hop(m).wait_recv()
            f_hop(micros + m, micros + m).wait_send()

        for cols in slices(hid, fb):
            qbuf[:, cols] = (slope[:, cols] * dot_nt(ebuf[m], wo[1, cols, :])).astype(BF16)
        for cols in slices(dim, nb):
            out = ebuf[m, :, cols].astype(F32) + dot_nt(qbuf[...], wi[1, cols, :])
            obuf[m, :, cols] = out.astype(BF16)

            @pl.when(jnp.logical_not(first))
            def _():
                b_hop(m, cols).start()

        @pl.when(first)
        def _():
            e_keep(m).start()
            e_push(m, 0).start()
            e_push(m, 1).start()

        grad_pass(h, ebuf.at[m], qbuf, a, gin, gout, h_next, wi.at[1], a_next, slope, fb)

    def step(t):
        m = t - micros - lag

        @pl.when(t == micros)
        def _():
            gin[...] = jnp.zeros_like(gin)
            gout[...] = jnp.zeros_like(gout)
            for c in w_copies(1):
                c.wait()

        @pl.when(t < 2 * micros)
        def _():
            fwd_unit(t, abuf.at[lax.rem(t + lag + micros + 1, 2)])

        @pl.when(m == -1)
        def _():
            act_pass(hbuf.at[micros], wi.at[1], abuf.at[0], slope, fb)

        @pl.when((m >= 0) & (m < micros))
        def _():
            bwd_unit(m)

    loop(0, 2 * micros + lag, step)

    outs = (pltpu.make_async_copy(gin, gin_hbm, o_sem.at[0]), pltpu.make_async_copy(gout, gout_hbm, o_sem.at[1]))
    for c in outs:
        c.start()

    def drain(m):
        h_keep(m).wait()
        h_push(m, 0).wait_send()
        h_push(m, 1).wait_send()
        h_forward(m, 0).wait_send()
        h_forward(m, 1).wait_send()
        h_whole(m).wait_recv()

        @pl.when(jnp.logical_not(first))
        def _():
            b_hop(m).wait_send()

        @pl.when(first)
        def _():
            e_keep(m).wait()
            for j in range(2):
                e_push(m, j).wait_send()
                e_push(m, j).wait_recv()

    loop(0, micros, drain)
    for c in outs:
        c.wait()


def run_front(stages, levels, x, g, w_in, w_out):
    micros, tokens, dim = x.shape
    _, _, hid = w_in.shape
    chunks = 3 if dim % 384 == 0 else 1
    dma = pltpu.SemaphoreType.DMA

    def rows(n):
        return jax.ShapeDtypeStruct((n * micros, tokens, dim), BF16)

    return pl.pallas_call(
        functools.partial(front_kernel, stages, levels, micros, chunks),
        out_shape=(rows(4), rows(1), rows(3), jax.ShapeDtypeStruct((dim, hid), F32), jax.ShapeDtypeStruct((hid, dim), F32)),
        in_specs=[ANY] * 4, out_specs=(ANY,) * 5,
        scratch_shapes=[
            pltpu.VMEM((2, dim, hid), BF16), pltpu.VMEM((2, hid, dim), BF16),
            pltpu.VMEM((2 * micros, tokens, dim), BF16), pltpu.VMEM((micros, tokens, dim), BF16), pltpu.VMEM((micros, tokens, dim), BF16),
            pltpu.VMEM((dim, hid), F32), pltpu.VMEM((hid, dim), F32),
            pltpu.VMEM((2, tokens, hid), BF16), pltpu.VMEM((tokens, hid), BF16), pltpu.VMEM((tokens, hid), F32),
            dma((2, 2)), dma((micros,)), dma((micros,)), dma((2 * micros,)), dma((2 * micros,)), dma((micros,)), dma((micros,)), dma((micros,)),
            dma((micros,)), dma((4, micros)), dma((3, micros)), dma((micros,)), dma((2, micros)), dma((2, micros)), dma((2,)),
        ],
        compiler_params=pltpu.CompilerParams(collective_id=0, has_side_effects=True, vmem_limit_bytes=VMEM_LIMIT),
        cost_estimate=pl.CostEstimate(flops=micros * 18 * tokens * dim * hid, bytes_accessed=8 * micros * tokens * dim * 2,
                                      transcendentals=3 * micros * tokens * hid),
        name='front',
    )(x, g, w_in, w_out)


def wide_kernel(stages, levels, micros, chunks, hall, eall, _, wi_hbm, wo_hbm, gin_hbm, gout_hbm, dx_out, y_out,
                wi, wo, hbuf, obuf, ebuf, gin, gout, abuf, qbuf, slope,
                w_sem, h_sem, n_send, b_send, b_recv, dx_sem, dx_send, dx_recv, y_send, y_recv, o_sem):
    s = lax.axis_index('stage')
    d = lax.axis_index('data')
    nxt, prv = lax.rem(s + 1, stages), lax.rem(s + stages - 1, stages)
    up, down = lax.rem(d + 1, levels), lax.rem(d + levels - 1, levels)
    dim, hid = wi.shape
    tokens = hbuf.shape[1]
    half = tokens // 2
    units = ebuf.shape[0]
    nb = dim // chunks
    fb = pick_block(hid, 768)
    hslots = hbuf.shape[0]
    first = s == 0
    last = s == stages - 1

    w_copies = (pltpu.make_async_copy(wi_hbm.at[0], wi, w_sem.at[0]), pltpu.make_async_copy(wo_hbm.at[0], wo, w_sem.at[1]))

    def h_copy(i):
        return pltpu.make_async_copy(hall.at[i], hbuf.at[lax.rem(i, hslots)], h_sem.at[lax.rem(i, hslots)])

    def entry(i):
        return pltpu.make_async_remote_copy(
            src_ref=eall.at[i], dst_ref=ebuf.at[i], send_sem=n_send.at[i], recv_sem=b_recv.at[i],
            device_id={'stage': prv}, device_id_type=MESH)

    def entry_far(m, j):
        rows = (slice(0, half), slice(half, tokens))[j]
        return pltpu.make_async_remote_copy(
            src_ref=eall.at[(2 - j) * micros + m, rows], dst_ref=ebuf.at[3 * micros + m, rows], send_sem=n_send.at[(3 + j) * micros + m],
            recv_sem=b_recv.at[3 * micros + m], device_id={'stage': prv, 'data': (up, down)[j]}, device_id_type=MESH)

    def b_hop(i, cols=slice(None)):
        o = lax.rem(i, micros)
        return pltpu.make_async_remote_copy(
            src_ref=obuf.at[o, :, cols], dst_ref=ebuf.at[i, :, cols], send_sem=b_send.at[o], recv_sem=b_recv.at[i],
            device_id={'stage': prv}, device_id_type=MESH)

    def dx_copy(m):
        return pltpu.make_async_copy(obuf.at[m], dx_out.at[m], dx_sem.at[m])

    def share(src, dst, send, recv, m, j):
        return pltpu.make_async_remote_copy(
            src_ref=src.at[m], dst_ref=dst.at[m], send_sem=send.at[m, j - 1], recv_sem=recv.at[m],
            device_id={'stage': lax.rem(s + j, stages)}, device_id_type=MESH)

    for c in w_copies:
        c.start()
    for i in range(hslots - 1):
        h_copy(i).start()

    signal_all([{'stage': lax.rem(s + step, stages)} for step in range(1, stages)]
               + [{'stage': st, 'data': lv} for st in (nxt, prv) for lv in (up, down)])

    @pl.when(first)
    def _():
        loop(0, 3 * micros, lambda i: entry(i).start())
        loop(0, micros, lambda m: entry_far(m, 0).start())
        loop(0, micros, lambda m: entry_far(m, 1).start())

    gin[...] = jnp.zeros_like(gin)
    gout[...] = jnp.zeros_like(gout)
    for c in w_copies:
        c.wait()
    h_copy(0).wait()
    act_pass(hbuf.at[0], wi, abuf.at[0], slope, fb)

    def unit(i):
        a, a_next = abuf.at[lax.rem(i, 2)], abuf.at[lax.rem(i + 1, 2)]
        h, h_next = hbuf.at[lax.rem(i, hslots)], hbuf.at[lax.rem(jnp.minimum(i + 1, units - 1), hslots)]
        o = lax.rem(i, micros)

        @pl.when(i + hslots - 1 < units)
        def _():
            h_copy(i + hslots - 1).start()

        b_hop(i).wait_recv()

        @pl.when(last & (i >= micros) & (i < 2 * micros))
        def _():
            for j in range(1, stages):
                share(y_out, y_out, y_send, y_recv, i - micros, j).start()

        @pl.when(jnp.logical_not(first) & (i >= micros))
        def _():
            b_hop(i - micros).wait_send()

        for cols in slices(hid, fb):
            qbuf[:, cols] = (slope[:, cols] * dot_nt(ebuf[i], wo[cols, :])).astype(BF16)

        @pl.when(jnp.logical_not(first) | (i < micros))
        def _():
            for cols in slices(dim, nb):
                out = ebuf[i, :, cols].astype(F32) + dot_nt(qbuf[...], wi[cols, :])
                obuf[o, :, cols] = out.astype(BF16)

                @pl.when(jnp.logical_not(first))
                def _():
                    b_hop(i, cols).start()

        @pl.when(first & (i < micros))
        def _():
            dx_copy(i).start()
            for j in range(1, stages):
                share(obuf, dx_out, dx_send, dx_recv, i, j).start()

        @pl.when(i + 1 < units)
        def _():
            h_copy(i + 1).wait()

        grad_pass(h, ebuf.at[i], qbuf, a, gin, gout, h_next, wi, a_next, slope, pick_block(hid, 256))

    loop(0, units, unit)

    outs = (pltpu.make_async_copy(gin, gin_hbm, o_sem.at[0]), pltpu.make_async_copy(gout, gout_hbm, o_sem.at[1]))
    for c in outs:
        c.start()

    @pl.when(first)
    def _():
        loop(0, 3 * micros, lambda i: entry(i).wait_send())
        loop(0, micros, lambda m: entry_far(m, 0).wait_send())
        loop(0, micros, lambda m: entry_far(m, 1).wait_send())
        loop(0, micros, lambda m: dx_copy(m).wait())
        for j in range(1, stages):
            loop(0, micros, lambda m, j=j: share(obuf, dx_out, dx_send, dx_recv, m, j).wait_send())

    @pl.when(jnp.logical_not(first))
    def _():
        loop(units - micros, units, lambda i: b_hop(i).wait_send())
        loop(0, micros, lambda m: share(obuf, dx_out, dx_send, dx_recv, m, 1).wait_recv())

    @pl.when(last)
    def _():
        for j in range(1, stages):
            loop(0, micros, lambda m, j=j: share(y_out, y_out, y_send, y_recv, m, j).wait_send())

    @pl.when(jnp.logical_not(last))
    def _():
        loop(0, micros, lambda m: share(y_out, y_out, y_send, y_recv, m, 1).wait_recv())

    for c in outs:
        c.wait()


def run_wide(stages, levels, micros, hall, eall, y, w_in, w_out):
    units, tokens, dim = hall.shape
    _, _, hid = w_in.shape
    chunks = 3 if dim % 384 == 0 else 1
    dma = pltpu.SemaphoreType.DMA
    small = jax.ShapeDtypeStruct((micros, tokens, dim), BF16)
    return pl.pallas_call(
        functools.partial(wide_kernel, stages, levels, micros, chunks),
        out_shape=(jax.ShapeDtypeStruct((dim, hid), F32), jax.ShapeDtypeStruct((hid, dim), F32), small, small),
        in_specs=[ANY] * 5, out_specs=(ANY,) * 4,
        scratch_shapes=[
            pltpu.VMEM((dim, hid), BF16), pltpu.VMEM((hid, dim), BF16),
            pltpu.VMEM((4, tokens, dim), BF16), pltpu.VMEM((micros, tokens, dim), BF16), pltpu.VMEM((units, tokens, dim), BF16),
            pltpu.VMEM((dim, hid), F32), pltpu.VMEM((hid, dim), F32),
            pltpu.VMEM((2, tokens, hid), BF16), pltpu.VMEM((tokens, hid), BF16), pltpu.VMEM((tokens, hid), F32),
            dma((2,)), dma((4,)), dma((5 * micros,)), dma((micros,)), dma((units,)), dma((micros,)), dma((micros, stages - 1)), dma((micros,)),
            dma((micros, stages - 1)), dma((micros,)), dma((2,)),
        ],
        input_output_aliases={2: 3},
        compiler_params=pltpu.CompilerParams(collective_id=1, has_side_effects=True, vmem_limit_bytes=VMEM_LIMIT),
        cost_estimate=pl.CostEstimate(flops=units * 10 * tokens * dim * hid, bytes_accessed=units * tokens * dim * 4,
                                      transcendentals=units * tokens * hid),
        name='wide',
    )(hall, eall, y, w_in, w_out)


def place_kernel(gin, gout, dx, y, gin_out, gout_out, dx_out, y_out):
    gin_out[0] = gin[...]
    gout_out[0] = gout[...]
    dx_out[...] = dx[...]
    y_out[...] = y[...]


def run_place(gin, gout, dx, y):
    dim, hid = gin.shape
    micros, tokens, _ = dx.shape
    small = pl.BlockSpec((1, tokens, dim), lambda i: (i, 0, 0))
    return pl.pallas_call(
        place_kernel, grid=(micros,),
        out_shape=(jax.ShapeDtypeStruct((2, dim, hid), F32), jax.ShapeDtypeStruct((2, hid, dim), F32),
                   jax.ShapeDtypeStruct(dx.shape, BF16), jax.ShapeDtypeStruct(y.shape, BF16)),
        in_specs=[pl.BlockSpec((dim // micros, hid), lambda i: (i, 0)), pl.BlockSpec((hid // micros, dim), lambda i: (i, 0)), small, small],
        out_specs=(pl.BlockSpec((1, dim // micros, hid), lambda i: (0, i, 0)), pl.BlockSpec((1, hid // micros, dim), lambda i: (0, i, 0)),
                   small, small),
        cost_estimate=pl.CostEstimate(flops=dim * hid, bytes_accessed=16 * dim * hid, transcendentals=0),
        name='place',
    )(gin, gout, dx, y)


def solution(mesh):
    stages, levels = mesh.shape['stage'], mesh.shape['data']

    def local_fn(x, g, w_in, w_out):
        wi, wo = w_in[:, 0], w_out[:, 0]
        hall, y, eall, gin_up, gout_up = run_front(stages, levels, x, g, wi, wo)
        gin_up, gout_up = lax.psum((gin_up, gout_up), 'data')
        gin_lo, gout_lo, dx, y = run_wide(stages, levels, x.shape[0], hall, eall, y, wi, wo)
        grad_in, grad_out, dx, y = run_place(gin_lo, gout_lo, dx, y)
        grad_in = lax.dynamic_update_slice(grad_in, gin_up[None], (1, 0, 0))
        grad_out = lax.dynamic_update_slice(grad_out, gout_up[None], (1, 0, 0))
        return y, dx, grad_in[:, None], grad_out[:, None]

    spec_rows = P(('part', 'data'))
    spec_weights = P(None, 'stage')
    spec_grads = P('part', 'stage')
    return jax.shard_map(local_fn, mesh=mesh, in_specs=(spec_rows, spec_rows, spec_weights, spec_weights), out_specs=(spec_rows, spec_rows, spec_grads, spec_grads), check_vma=False)
```

time: 2210 us -> 677 us (0.31)
  waiting for transfers between devices: 1070 us -> 0.06 us
  Pallas kernels: 0 us -> 650 us
  matrix products: 505 us -> 0 us
  starting transfers between devices: 289 us -> 0.06 us
  local copies, waits for them, and re-layouts: 272 us -> 13.1 us
  other arithmetic: 56.2 us -> 0 us
    psum x2 -> x1, waiting for transfers between devices: 710 us -> 0.01 us  [local_fn(): gin_up, gout_up = lax.psum((gin_up, gout_up), 'data')]
    pallas_call x0 -> x3, Pallas kernels: none -> 650 us  [the longest x1 355 us: run_wide(): pl.pallas_call(functools.partial(wide_kernel, stages, levels, micros, chu...]
    dot_general x96 -> x0, matrix products: 505 us -> none  [the longest x16 128 us: layer_backward(): jnp.einsum('tf,td->fd', hidden, g_next, preferred_element_type=jnp.float32)]
    ppermute x46 -> x0, waiting for transfers between devices: 360 us -> none  [the longest x23 238 us: fwd_tick(): return (lax.ppermute(h_out, 'stage', to_next), h_saved, pre_saved, y_buf)]
    ppermute x46 -> x0, starting transfers between devices: 289 us -> none  [the longest x23 285 us: bwd_tick(): lax.ppermute(g_prev, 'stage', to_prev)]
    dynamic_slice x48 -> x0, local copies, waits for them, and re-layouts: 166 us -> none  [pick_row(): return lax.dynamic_index_in_dim(stacked, row_idx, 0, keepdims=False)]
    broadcast_in_dim x4 -> x0, local copies, waits for them, and re-layouts: 36.8 us -> none  [the longest x1 16.3 us: local_fn(): jnp.zeros((unit_count, tokens, hidden_dim), jnp.float32)]
    dynamic_update_slice x16 -> x0, other arithmetic: 32.5 us -> none  [put_row(): return lax.dynamic_update_index_in_dim(stacked, row_val, row_idx, 0)]
  transfers between devices with their start and end apart: 48 -> 1, of which waited for: 48 -> 0; matrix products, arithmetic and copies ran while one was open for 0% -> 0% of each run, Pallas kernels for 0% -> 55%
where the time goes in v2:
time: 677 us
  Pallas kernels  650 us (96%)
  between operations  14.1 us (2%)
  local copies, waits for them, and re-layouts  13.1 us (2%)
    pallas_call x1, Pallas kernels, run_wide(): pl.pallas_call(functools.partial(wide_kernel, stages, levels, micros, chu...  355 us
    pallas_call x1, Pallas kernels, run_front(): pl.pallas_call(functools.partial(front_kernel, stages, levels, micros, ch...  277 us
    pallas_call x1, Pallas kernels, run_place(): pl.pallas_call(place_kernel, grid=(micros,), out_shape=(jax.ShapeDtypeStr...  17.9 us
  transfers between devices with their start and end apart: 1, of which 0 were waited for; matrix products, arithmetic and copies ran while one was open for 0% of the time, Pallas kernels for 55%

profile of v2, /device:TPU:96, one launch (start us, length us, event | category | flops | bytes accessed | tf_op | source)
XLA Modules:
  0.0 677.4 jit_solution(12830835412577331675)
XLA Ops:
  7.2 0.1 all-reduce.3.cloned.1.call-start
  7.2 276.8 %front.1 = (bf16[32,256,768]{2,1,0:T(8,128)(2,1)}, bf16[8,256,768]{2,1,0:T(8,128)(2,1)}, bf16[24,256,768]{2,1,0:T(8,128)(2,1)}, f32[768,3072]{1,0:T(8,128)}, f32[3072,768]{1,0:T(8,128)}) custom-call(bf16[8,256,768]{2,1,0:T(8,128)(2,1)} %x_hbm.1, bf16[8,256,768]{2,1,0:T(8,128)(2,1)} %g_hbm.1, bf16[2,768,3072]{2,1,0:T(8,128)(2,1)} %bitcast.14, ...), custom_call_target="tpu_custom_call" | custom-call | flops 86973087744 | bytes 25165824 | tf_op jit(solution)/shard_map/front/pallas_call | solution.py:302
  284.0 0.1 all-reduce.3.cloned.1.call-update
  284.1 355.4 %wide.1 = (f32[768,3072]{1,0:T(8,128)}, f32[3072,768]{1,0:T(8,128)}, bf16[8,256,768]{2,1,0:T(8,128)(2,1)}, bf16[8,256,768]{2,1,0:T(8,128)(2,1)}) custom-call(bf16[32,256,768]{2,1,0:T(8,128)(2,1)} %get-tuple-element.17.hall, bf16[24,256,768]{2,1,0:T(8,128)(2,1)} %get-tuple-element.18.eall, ...), custom_call_target="tpu_custom_call", output_to_operand_aliasing={{3}: (2, {})} | custom-call | flops 193273528320 | bytes 25165824 | tf_op jit(solution)/shard_map/wide/pallas_call | solution.py:473
  639.4 17.9 %place.1 = (f32[2,768,3072]{2,1,0:T(8,128)}, f32[2,3072,768]{2,1,0:T(8,128)}, bf16[8,256,768]{2,1,0:T(8,128)(2,1)}, bf16[8,256,768]{2,1,0:T(8,128)(2,1)}) custom-call(f32[768,3072]{1,0:T(8,128)} %get-tuple-element.20.gin, f32[3072,768]{1,0:T(8,128)} %get-tuple-element.21.gout, bf16[8,256,768]{2,1,0:T(8,128)(2,1)} %get-tuple-element.22.dx, ...), custom_call_target="tpu_custom_call" | custom-call | flops 2359296 | bytes 37748736 | tf_op jit(solution)/shard_map/place/pallas_call | solution.py:504
  657.4 0.0 all-reduce.3.cloned.1.call-done
  657.4 0.0 copy-start
  657.4 8.8 %constant_dynamic-update-slice_fusion.1 = f32[2,1,768,3072]{3,2,0,1:T(8,128)} fusion(f32[2,1,768,3072]{3,2,0,1:T(8,128)} %bitcast.12, f32[1,1,768,3072]{3,2,0,1:T(8,128)} %get-tuple-element.34), kind=kLoop, calls=%fused_computation.1 | loop fusion | bytes 18874368 | tf_op jit(solution)/shard_map/dynamic_update_slice | solution.py:525
  666.1 0.0 copy-done
  666.1 4.3 constant_dynamic-update-slice_fusion
Async XLA Ops:
  7.2 650.2 %all-reduce.3.cloned.1.call-start = ((), (), s32[]{:S(2)}) async-start(), calls=%async_computation | async-start | bytes 37748736 | tf_op jit(solution)/shard_map/psum | solution.py:522
  657.4 8.8 %copy-start = (f32[1,1,3072,768]{3,2,0,1:T(8,128)S(1)}, f32[1,1,3072,768]{3,2,0,1:T(8,128)}, u32[]{:S(2)}) copy-start(f32[1,1,3072,768]{3,2,0,1:T(8,128)} %get-tuple-element.35) | copy-start | bytes 28311556
Sparse Core Ops, SparseCore 0:
  284.2 343.2 all-reduce.2

commit v3 on v2

v3 whole, which is shorter than its diff:
```python
import functools
import jax
import jax.numpy as jnp
from jax import lax
from jax.experimental import pallas as pl
from jax.experimental.pallas import tpu as pltpu
from jax.sharding import PartitionSpec as P

MESH = pl.DeviceIdType.MESH
F32 = jnp.float32
BF16 = jnp.bfloat16
ANY = pl.BlockSpec(memory_space=pl.ANY)
GELU_A = 0.7978845608028654
GELU_B = 0.044715
VMEM_LIMIT = 66_000_000


def dot(a, b):
    return jnp.dot(a, b, preferred_element_type=F32)


def dot_nt(a, b):
    return lax.dot_general(a, b, (((1,), (1,)), ((), ())), preferred_element_type=F32)


def dot_tn(a, b):
    return lax.dot_general(a, b, (((0,), (0,)), ((), ())), preferred_element_type=F32)


def gelu_only(z):
    t = jnp.tanh(z * (GELU_A + (GELU_A * GELU_B) * (z * z)))
    return z * (0.5 * t + 0.5)


def gelu_and_slope(z):
    s = (GELU_A * GELU_B) * (z * z)
    cdf = 0.5 * jnp.tanh(z * (GELU_A + s)) + 0.5
    a = z * cdf
    return a, cdf + (a * (1.0 - cdf)) * (2.0 * GELU_A + 6.0 * s)


def pick_block(size, target):
    block = min(size, target)
    while size % block:
        block //= 2
    return block


def loop(lo, hi, fn):
    def body(i, _):
        fn(i)
        return 0
    lax.fori_loop(lo, hi, body, 0)


def signal_all(targets):
    sem = pltpu.get_barrier_semaphore()
    for target in targets:
        pl.semaphore_signal(sem, inc=1, device_id=target, device_id_type=MESH)
    pl.semaphore_wait(sem, len(targets))


def slices(size, block):
    return [slice(b * block, (b + 1) * block) for b in range(size // block)]


def act_pass(h, wi, a, slope, fb):
    for cols in slices(wi.shape[1], fb):
        act, der = gelu_and_slope(dot(h[...], wi[:, cols]))
        a[:, cols] = act.astype(BF16)
        slope[:, cols] = der


def front_kernel(stages, levels, micros, chunks, x_hbm, g_hbm, wi_hbm, wo_hbm, hall, y_out, eall, gin_hbm, gout_hbm, aup, qup,
                 wi, wo, hbuf, obuf, ebuf, gin, gout, abuf, qbuf, slope,
                 w_sem, x_sem, g_sem, f_send, f_recv, b_send, b_recv, y_sem, h_save, h_send, h_recv, e_save, e_send, e_recv,
                 a_save, a_load, o_sem):
    s = lax.axis_index('stage')
    d = lax.axis_index('data')
    nxt, prv = lax.rem(s + 1, stages), lax.rem(s + stages - 1, stages)
    up, down = lax.rem(d + 1, levels), lax.rem(d + levels - 1, levels)
    _, dim, hid = wi.shape
    tokens = hbuf.shape[1]
    half = tokens // 2
    nb = dim // chunks
    fb = pick_block(hid, 768)
    wb = pick_block(hid, 512)
    first = s == 0
    last = s == stages - 1
    inner = jnp.logical_not(last)
    lag = jnp.minimum(3 * (stages - 1 - s), micros)
    defer = s >= stages - 2

    def w_copies(v):
        return (pltpu.make_async_copy(wi_hbm.at[v], wi.at[v], w_sem.at[v, 0]),
                pltpu.make_async_copy(wo_hbm.at[v], wo.at[v], w_sem.at[v, 1]))

    def x_copy(m):
        return pltpu.make_async_copy(x_hbm.at[m], hbuf.at[m], x_sem.at[m])

    def g_copy(m):
        return pltpu.make_async_copy(g_hbm.at[m], ebuf.at[m], g_sem.at[m])

    def f_hop(i, slot, cols=slice(None)):
        return pltpu.make_async_remote_copy(
            src_ref=obuf.at[lax.rem(i, micros), :, cols], dst_ref=hbuf.at[slot, :, cols], send_sem=f_send.at[i], recv_sem=f_recv.at[slot],
            device_id={'stage': nxt}, device_id_type=MESH)

    def b_hop(m, cols=slice(None)):
        return pltpu.make_async_remote_copy(
            src_ref=obuf.at[m, :, cols], dst_ref=ebuf.at[m, :, cols], send_sem=b_send.at[m], recv_sem=b_recv.at[m],
            device_id={'stage': prv}, device_id_type=MESH)

    def y_copy(m):
        return pltpu.make_async_copy(obuf.at[m], y_out.at[m], y_sem.at[m])

    def h_keep(m):
        return pltpu.make_async_copy(hbuf.at[m], hall.at[m], h_save.at[m])

    def h_push(m, j):
        return pltpu.make_async_remote_copy(
            src_ref=hbuf.at[m], dst_ref=hall.at[(2 - j) * micros + m], send_sem=h_send.at[j, m], recv_sem=h_recv.at[1 - j, m],
            device_id={'data': (up, down)[j]}, device_id_type=MESH)

    def h_forward(m, j):
        rows = (slice(0, half), slice(half, tokens))[j]
        return pltpu.make_async_remote_copy(
            src_ref=hall.at[(2 - j) * micros + m, rows], dst_ref=hall.at[3 * micros + m, rows], send_sem=h_send.at[2 + j, m],
            recv_sem=h_recv.at[2, m], device_id={'data': (up, down)[j]}, device_id_type=MESH)

    def h_whole(m):
        return pltpu.make_async_remote_copy(
            src_ref=hall.at[m], dst_ref=hall.at[3 * micros + m], send_sem=h_send.at[2, m], recv_sem=h_recv.at[2, m],
            device_id={'data': up}, device_id_type=MESH)

    def e_keep(m):
        return pltpu.make_async_copy(obuf.at[m], eall.at[m], e_save.at[m])

    def e_push(m, j, cols=slice(None)):
        return pltpu.make_async_remote_copy(
            src_ref=obuf.at[m, :, cols], dst_ref=eall.at[(2 - j) * micros + m, :, cols], send_sem=e_send.at[j, m], recv_sem=e_recv.at[1 - j, m],
            device_id={'data': (up, down)[j]}, device_id_type=MESH)

    def e_forward(m, j):
        rows = (slice(0, half), slice(half, tokens))[j]
        return pltpu.make_async_remote_copy(
            src_ref=eall.at[(2 - j) * micros + m, rows], dst_ref=eall.at[3 * micros + m, rows], send_sem=e_send.at[2 + j, m],
            recv_sem=e_recv.at[2, m], device_id={'data': (up, down)[j]}, device_id_type=MESH)

    def e_whole(m):
        return pltpu.make_async_remote_copy(
            src_ref=eall.at[m], dst_ref=eall.at[3 * micros + m], send_sem=e_send.at[2, m], recv_sem=e_recv.at[2, m],
            device_id={'data': up}, device_id_type=MESH)

    def a_keep(m):
        return pltpu.make_async_copy(abuf.at[lax.rem(m, 2)], aup.at[m], a_save.at[0, m])

    def q_keep(m):
        return pltpu.make_async_copy(qbuf.at[lax.rem(m, 2)], qup.at[m], a_save.at[1, m])

    def loads(m):
        k = lax.rem(m, 2)
        return (pltpu.make_async_copy(aup.at[m], abuf.at[k], a_load.at[0, k]), pltpu.make_async_copy(qup.at[m], qbuf.at[k], a_load.at[1, k]))

    for v in range(2):
        for c in w_copies(v):
            c.start()

    @pl.when(first)
    def _():
        loop(0, micros, lambda m: x_copy(m).start())

    @pl.when(last)
    def _():
        loop(0, micros, lambda m: g_copy(m).start())

    signal_all([{'stage': lax.rem(s + step, stages)} for step in range(1, stages)] + [{'data': up}, {'data': down}])

    for c in w_copies(0):
        c.wait()

    def fwd_wait(i):
        lower = i < micros

        @pl.when(first & lower)
        def _():
            x_copy(i).wait()

        @pl.when(jnp.logical_not(first & lower))
        def _():
            f_hop(i, i).wait_recv()

    def fwd_unit(i, aslot):
        v = i // micros
        lower = i < micros
        upper = jnp.logical_not(lower)
        o = lax.rem(i, micros)
        slot = jnp.where(last, i + micros, i)
        final = last & upper
        a = abuf.at[aslot]

        @pl.when(lower)
        def _():
            h_keep(i).start()
            h_push(i, 0).start()
            h_push(i, 1).start()

        @pl.when(upper)
        def _():
            f_hop(o, o).wait_send()
            h_push(o, 0).wait_recv()
            h_push(o, 1).wait_recv()
            h_forward(o, 0).start()
            h_forward(o, 1).start()

        @pl.when(jnp.logical_not(final))
        def _():
            for cols in slices(hid, fb):
                a[:, cols] = gelu_only(dot(hbuf[i], wi[v, :, cols])).astype(BF16)

        for cols in slices(dim, nb):
            out = hbuf[i, :, cols].astype(F32) + dot(a[...], wo[v, :, cols])
            obuf[o, :, cols] = out.astype(BF16)

            @pl.when(jnp.logical_not(final))
            def _():
                f_hop(i, slot, cols).start()

        @pl.when(final)
        def _():
            y_copy(o).start()

    def bwd_unit(m):
        q = qbuf.at[lax.rem(m, 2)]

        @pl.when(last)
        def _():
            g_copy(m).wait()
            y_copy(m).wait()

        @pl.when(inner)
        def _():
            b_hop(m).wait_recv()
            f_hop(micros + m, micros + m).wait_send()

        @pl.when(defer & (m >= 2))
        def _():
            q_keep(m - 2).wait()

        for cols in slices(hid, fb):
            q[:, cols] = (slope[:, cols] * dot_nt(ebuf[m], wo[1, cols, :])).astype(BF16)
        for cols in slices(dim, nb):
            out = ebuf[m, :, cols].astype(F32) + dot_nt(q[...], wi[1, cols, :])
            obuf[m, :, cols] = out.astype(BF16)

            @pl.when(jnp.logical_not(first))
            def _():
                b_hop(m, cols).start()

            @pl.when(first)
            def _():
                e_push(m, 0, cols).start()
                e_push(m, 1, cols).start()

        @pl.when(first)
        def _():
            e_keep(m).start()

            @pl.when(m >= 1)
            def _():
                far(m - 1)

        @pl.when(defer)
        def _():
            q_keep(m).start()

    def far(m):
        for j in range(2):
            e_push(m, j).wait_recv()
        for j in range(2):
            e_forward(m, j).start()

    def weight_unit(m):
        k = lax.rem(m, 2)
        for cols in slices(hid, wb):
            gin[:, cols] += dot_tn(hbuf[micros + m], qbuf[k, :, cols])
            gout[cols, :] += dot_tn(abuf[k, :, cols], ebuf[m])

    def step(t):
        m = t - micros - lag
        active = (m >= 0) & (m < micros)
        put_off = m - micros
        w = jnp.where(defer, put_off, m)

        @pl.when(t == micros)
        def _():
            gin[...] = jnp.zeros_like(gin)
            gout[...] = jnp.zeros_like(gout)
            for c in w_copies(1):
                c.wait()

        early = last & active

        @pl.when(early)
        def _():
            fwd_wait(t)

        @pl.when(active)
        def _():
            @pl.when(defer & (m >= 2))
            def _():
                a_keep(m - 2).wait()

            act_pass(hbuf.at[micros + m], wi.at[1], abuf.at[lax.rem(m, 2)], slope, fb)

            @pl.when(defer)
            def _():
                a_keep(m).start()

        @pl.when(t < 2 * micros)
        def _():
            @pl.when(jnp.logical_not(early))
            def _():
                fwd_wait(t)

            fwd_unit(t, jnp.where(early, lax.rem(t + micros, 2), 2))

        @pl.when(active)
        def _():
            bwd_unit(m)

        @pl.when(put_off == 0)
        def _():
            for n in range(micros - 2, micros):
                a_keep(n).wait()
                q_keep(n).wait()
            for c in loads(0):
                c.start()

        @pl.when((put_off >= 0) & (put_off < micros - 1))
        def _():
            for c in loads(put_off + 1):
                c.start()

        @pl.when(put_off >= 0)
        def _():
            for c in loads(put_off):
                c.wait()

        @pl.when((w >= 0) & (w < micros))
        def _():
            weight_unit(w)

    loop(0, 2 * micros + lag + jnp.where(defer, micros, 0), step)

    outs = (pltpu.make_async_copy(gin, gin_hbm, o_sem.at[0]), pltpu.make_async_copy(gout, gout_hbm, o_sem.at[1]))
    for c in outs:
        c.start()

    @pl.when(first)
    def _():
        far(micros - 1)

    def drain(m):
        h_keep(m).wait()
        h_push(m, 0).wait_send()
        h_push(m, 1).wait_send()
        h_forward(m, 0).wait_send()
        h_forward(m, 1).wait_send()
        h_whole(m).wait_recv()

        @pl.when(jnp.logical_not(first))
        def _():
            b_hop(m).wait_send()

        @pl.when(first)
        def _():
            e_keep(m).wait()
            for j in range(2):
                e_push(m, j).wait_send()
                e_forward(m, j).wait_send()
            e_whole(m).wait_recv()

    loop(0, micros, drain)
    for c in outs:
        c.wait()


def run_front(stages, levels, x, g, w_in, w_out):
    micros, tokens, dim = x.shape
    _, _, hid = w_in.shape
    chunks = 3 if dim % 384 == 0 else 1
    dma = pltpu.SemaphoreType.DMA

    def rows(n):
        return jax.ShapeDtypeStruct((n * micros, tokens, dim), BF16)

    acts = jax.ShapeDtypeStruct((micros, tokens, hid), BF16)
    return pl.pallas_call(
        functools.partial(front_kernel, stages, levels, micros, chunks),
        out_shape=(rows(4), rows(1), rows(4), jax.ShapeDtypeStruct((dim, hid), F32), jax.ShapeDtypeStruct((hid, dim), F32), acts, acts),
        in_specs=[ANY] * 4, out_specs=(ANY,) * 7,
        scratch_shapes=[
            pltpu.VMEM((2, dim, hid), BF16), pltpu.VMEM((2, hid, dim), BF16),
            pltpu.VMEM((2 * micros, tokens, dim), BF16), pltpu.VMEM((micros, tokens, dim), BF16), pltpu.VMEM((micros, tokens, dim), BF16),
            pltpu.VMEM((dim, hid), F32), pltpu.VMEM((hid, dim), F32),
            pltpu.VMEM((3, tokens, hid), BF16), pltpu.VMEM((2, tokens, hid), BF16), pltpu.VMEM((tokens, hid), F32),
            dma((2, 2)), dma((micros,)), dma((micros,)), dma((2 * micros,)), dma((2 * micros,)), dma((micros,)), dma((micros,)), dma((micros,)),
            dma((micros,)), dma((4, micros)), dma((3, micros)), dma((micros,)), dma((4, micros)), dma((3, micros)),
            dma((2, micros)), dma((2, 2)), dma((2,)),
        ],
        compiler_params=pltpu.CompilerParams(collective_id=0, has_side_effects=True, vmem_limit_bytes=VMEM_LIMIT),
        cost_estimate=pl.CostEstimate(flops=micros * 18 * tokens * dim * hid, bytes_accessed=4 * micros * tokens * hid * 2,
                                      transcendentals=3 * micros * tokens * hid),
        name='front',
    )(x, g, w_in, w_out)


def wide_kernel(stages, micros, chunks, hall, eall, _, wi_hbm, wo_hbm, a_out, q_out, e_out, dx_out, y_out,
                wi, wo, hbuf, obuf, ebuf, abuf, qbuf,
                w_sem, h_sem, n_send, b_send, b_recv, dx_sem, dx_send, dx_recv, y_send, y_recv, s_sem):
    s = lax.axis_index('stage')
    nxt, prv = lax.rem(s + 1, stages), lax.rem(s + stages - 1, stages)
    dim, hid = wi.shape
    units = ebuf.shape[0]
    nb = dim // chunks
    fb = pick_block(hid, 768)
    hslots = hbuf.shape[0]
    first = s == 0
    last = s == stages - 1

    w_copies = (pltpu.make_async_copy(wi_hbm.at[0], wi, w_sem.at[0]), pltpu.make_async_copy(wo_hbm.at[0], wo, w_sem.at[1]))

    def h_copy(i):
        return pltpu.make_async_copy(hall.at[i], hbuf.at[lax.rem(i, hslots)], h_sem.at[lax.rem(i, hslots)])

    def entry(i):
        return pltpu.make_async_remote_copy(
            src_ref=eall.at[i], dst_ref=ebuf.at[i], send_sem=n_send.at[i], recv_sem=b_recv.at[i],
            device_id={'stage': prv}, device_id_type=MESH)

    def b_hop(i, cols=slice(None)):
        o = lax.rem(i, micros)
        return pltpu.make_async_remote_copy(
            src_ref=obuf.at[o, :, cols], dst_ref=ebuf.at[i, :, cols], send_sem=b_send.at[o], recv_sem=b_recv.at[i],
            device_id={'stage': prv}, device_id_type=MESH)

    def dx_copy(m):
        return pltpu.make_async_copy(obuf.at[m], dx_out.at[m], dx_sem.at[m])

    def dx_hop(m, src):
        return pltpu.make_async_remote_copy(
            src_ref=src.at[m], dst_ref=dx_out.at[m], send_sem=dx_send.at[m], recv_sem=dx_recv.at[m],
            device_id={'stage': nxt}, device_id_type=MESH)

    def y_hop(m):
        return pltpu.make_async_remote_copy(
            src_ref=y_out.at[m], dst_ref=y_out.at[m], send_sem=y_send.at[m], recv_sem=y_recv.at[m],
            device_id={'stage': nxt}, device_id_type=MESH)

    def relay(i):
        my = jnp.where(last, i - 1, i - 2 - 3 * s)
        mx = i - 1 - 3 * s

        @pl.when((my >= 0) & (my < micros))
        def _():
            @pl.when(jnp.logical_not(last))
            def _():
                y_hop(my).wait_recv()

            @pl.when(s != stages - 2)
            def _():
                y_hop(my).start()

        @pl.when((mx >= 0) & (mx < micros) & jnp.logical_not(first))
        def _():
            dx_hop(mx, dx_out).wait_recv()

            @pl.when(jnp.logical_not(last))
            def _():
                dx_hop(mx, dx_out).start()

    def keep(i):
        k = lax.rem(i, 2)
        return (pltpu.make_async_copy(abuf.at[k], a_out.at[i], s_sem.at[0, k]), pltpu.make_async_copy(qbuf.at[k], q_out.at[i], s_sem.at[1, k]),
                pltpu.make_async_copy(ebuf.at[i], e_out.at[i], s_sem.at[2, k]))

    for c in w_copies:
        c.start()
    for i in range(hslots - 1):
        h_copy(i).start()

    signal_all([{'stage': lax.rem(s + step, stages)} for step in range(1, stages)])

    @pl.when(first)
    def _():
        loop(0, units, lambda i: entry(i).start())

    for c in w_copies:
        c.wait()

    def unit(i):
        k = lax.rem(i, 2)
        a, q, h = abuf.at[k], qbuf.at[k], hbuf.at[lax.rem(i, hslots)]
        o = lax.rem(i, micros)

        @pl.when(i + hslots - 1 < units)
        def _():
            h_copy(i + hslots - 1).start()

        h_copy(i).wait()
        b_hop(i).wait_recv()

        @pl.when(i >= 2)
        def _():
            for c in keep(i - 2):
                c.wait()

        relay(i)

        @pl.when(jnp.logical_not(first) & (i >= micros))
        def _():
            b_hop(i - micros).wait_send()

        for cols in slices(hid, fb):
            act, der = gelu_and_slope(dot(h[...], wi[:, cols]))
            a[:, cols] = act.astype(BF16)
            q[:, cols] = (der * dot_nt(ebuf[i], wo[cols, :])).astype(BF16)

        @pl.when(jnp.logical_not(first) | (i < micros))
        def _():
            for cols in slices(dim, nb):
                out = ebuf[i, :, cols].astype(F32) + dot_nt(q[...], wi[cols, :])
                obuf[o, :, cols] = out.astype(BF16)

                @pl.when(jnp.logical_not(first))
                def _():
                    b_hop(i, cols).start()

        @pl.when(first & (i < micros))
        def _():
            dx_copy(i).start()
            dx_hop(i, obuf).start()

        for c in keep(i):
            c.start()

    loop(0, units, unit)
    loop(units, max(units, micros + 3 * stages - 2), relay)

    @pl.when(first)
    def _():
        loop(0, units, lambda i: entry(i).wait_send())
        loop(0, micros, lambda m: dx_copy(m).wait())

    @pl.when(jnp.logical_not(first))
    def _():
        loop(units - micros, units, lambda i: b_hop(i).wait_send())

    @pl.when(jnp.logical_not(last))
    def _():
        loop(0, micros, lambda m: dx_hop(m, dx_out).wait_send())

    @pl.when(s != stages - 2)
    def _():
        loop(0, micros, lambda m: y_hop(m).wait_send())

    for i in (units - 2, units - 1):
        for c in keep(i):
            c.wait()


def run_wide(stages, micros, hall, eall, y, w_in, w_out):
    units, tokens, dim = hall.shape
    _, _, hid = w_in.shape
    chunks = 3 if dim % 384 == 0 else 1
    dma = pltpu.SemaphoreType.DMA
    small = jax.ShapeDtypeStruct((micros, tokens, dim), BF16)
    acts = jax.ShapeDtypeStruct((units, tokens, hid), BF16)
    return pl.pallas_call(
        functools.partial(wide_kernel, stages, micros, chunks),
        out_shape=(acts, acts, jax.ShapeDtypeStruct((units, tokens, dim), BF16), small, small),
        in_specs=[ANY] * 5, out_specs=(ANY,) * 5,
        scratch_shapes=[
            pltpu.VMEM((dim, hid), BF16), pltpu.VMEM((hid, dim), BF16),
            pltpu.VMEM((4, tokens, dim), BF16), pltpu.VMEM((micros, tokens, dim), BF16), pltpu.VMEM((units, tokens, dim), BF16),
            pltpu.VMEM((2, tokens, hid), BF16), pltpu.VMEM((2, tokens, hid), BF16),
            dma((2,)), dma((4,)), dma((units,)), dma((micros,)), dma((units,)), dma((micros,)), dma((micros,)), dma((micros,)),
            dma((micros,)), dma((micros,)), dma((3, 2)),
        ],
        input_output_aliases={2: 4},
        compiler_params=pltpu.CompilerParams(collective_id=1, has_side_effects=True, vmem_limit_bytes=VMEM_LIMIT),
        cost_estimate=pl.CostEstimate(flops=units * 6 * tokens * dim * hid, bytes_accessed=units * tokens * hid * 4,
                                      transcendentals=units * tokens * hid),
        name='wide',
    )(hall, eall, y, w_in, w_out)


def wgrad_kernel(lhs, rhs, out):
    @pl.when(pl.program_id(1) == 0)
    def _():
        out[...] = jnp.zeros_like(out)

    out[0] += dot_tn(lhs[...], rhs[...])


def run_wgrad(lhs, rhs, split_lhs, name):
    lhs, rhs = lhs.reshape(-1, lhs.shape[-1]), rhs.reshape(-1, rhs.shape[-1])
    tokens, m, n = lhs.shape[0], lhs.shape[1], rhs.shape[1]
    kb = pick_block(tokens, 2048)
    fb = pick_block(m if split_lhs else n, 1024)
    if split_lhs:
        grid, block = (m // fb, tokens // kb), (1, fb, n)
        lhs_spec, rhs_spec = pl.BlockSpec((kb, fb), lambda j, k: (k, j)), pl.BlockSpec((kb, n), lambda j, k: (k, 0))
        place = lambda j, k: (0, j, 0)
    else:
        grid, block = (n // fb, tokens // kb), (1, m, fb)
        lhs_spec, rhs_spec = pl.BlockSpec((kb, m), lambda j, k: (k, 0)), pl.BlockSpec((kb, fb), lambda j, k: (k, j))
        place = lambda j, k: (0, 0, j)
    return pl.pallas_call(
        wgrad_kernel, grid=grid, out_shape=jax.ShapeDtypeStruct((2, m, n), F32), in_specs=[lhs_spec, rhs_spec],
        out_specs=pl.BlockSpec(block, place), compiler_params=pltpu.CompilerParams(vmem_limit_bytes=VMEM_LIMIT),
        cost_estimate=pl.CostEstimate(flops=2 * tokens * m * n, bytes_accessed=2 * tokens * (m + n) + 4 * m * n, transcendentals=0),
        name=name,
    )(lhs, rhs)


def place_kernel(dx, y, dx_out, y_out):
    dx_out[...] = dx[...]
    y_out[...] = y[...]


def run_place(dx, y):
    spec = pl.BlockSpec((1,) + dx.shape[1:], lambda i: (i, 0, 0))
    shape = jax.ShapeDtypeStruct(dx.shape, BF16)
    return pl.pallas_call(
        place_kernel, grid=(dx.shape[0],), out_shape=(shape, shape), in_specs=[spec] * 2, out_specs=(spec, spec),
        cost_estimate=pl.CostEstimate(flops=dx.size, bytes_accessed=8 * dx.size, transcendentals=0), name='place',
    )(dx, y)


def solution(mesh):
    stages, levels = mesh.shape['stage'], mesh.shape['data']

    def local_fn(x, g, w_in, w_out):
        wi, wo = w_in[:, 0], w_out[:, 0]
        hall, y, eall, gin_up, gout_up, _, _ = run_front(stages, levels, x, g, wi, wo)
        gin_up, gout_up = lax.psum((gin_up, gout_up), 'data')
        alow, qlow, elow, dx, y = run_wide(stages, x.shape[0], hall, eall, y, wi, wo)
        grad_in = run_wgrad(hall, qlow, False, 'gin_low')
        grad_out = run_wgrad(alow, elow, True, 'gout_low')
        dx, y = run_place(dx, y)
        grad_in = lax.dynamic_update_slice(grad_in, gin_up[None], (1, 0, 0))
        grad_out = lax.dynamic_update_slice(grad_out, gout_up[None], (1, 0, 0))
        return y, dx, grad_in[:, None], grad_out[:, None]

    spec_rows = P(('part', 'data'))
    spec_weights = P(None, 'stage')
    spec_grads = P('part', 'stage')
    return jax.shard_map(local_fn, mesh=mesh, in_specs=(spec_rows, spec_rows, spec_weights, spec_weights), out_specs=(spec_rows, spec_rows, spec_grads, spec_grads), check_vma=False)
```

time: 677 us -> 666 us (0.984)
  Pallas kernels: 650 us -> 639 us
    pallas_call x1, Pallas kernels: 277 us -> 261 us  [run_front(): pl.pallas_call(functools.partial(front_kernel, stages, levels, micros, ch...]
    pallas_call x2 -> x4, Pallas kernels: 373 us -> 377 us  [the longest x1 272 us: run_wide(): pl.pallas_call(functools.partial(wide_kernel, stages, micros, chunks), ou...]
  transfers between devices with their start and end apart: 1 -> 1, of which waited for: 0 -> 0; matrix products, arithmetic and copies ran while one was open for 0% -> 0% of each run, Pallas kernels for 55% -> 57%
where the time goes in v3:
time: 666 us
  Pallas kernels  639 us (96%)
  between operations  14.1 us (2%)
  local copies, waits for them, and re-layouts  13.1 us (2%)
    pallas_call x1, Pallas kernels, run_wide(): pl.pallas_call(functools.partial(wide_kernel, stages, micros, chunks), ou...  272 us
    pallas_call x1, Pallas kernels, run_front(): pl.pallas_call(functools.partial(front_kernel, stages, levels, micros, ch...  261 us
    pallas_call x2, Pallas kernels, run_wgrad(): pl.pallas_call(wgrad_kernel, grid=grid, out_shape=jax.ShapeDtypeStruct((2...  97.6 us
  transfers between devices with their start and end apart: 1, of which 0 were waited for; matrix products, arithmetic and copies ran while one was open for 0% of the time, Pallas kernels for 57%

profile of v3, /device:TPU:96, one launch (start us, length us, event | category | flops | bytes accessed | tf_op | source)
XLA Modules:
  0.0 665.9 jit_solution(14546701941360119631)
XLA Ops:
  7.2 0.1 all-reduce.3.cloned.1.call-start
  7.2 261.2 %front.1 = (bf16[32,256,768]{2,1,0:T(8,128)(2,1)}, bf16[8,256,768]{2,1,0:T(8,128)(2,1)}, bf16[32,256,768]{2,1,0:T(8,128)(2,1)}, f32[768,3072]{1,0:T(8,128)}, f32...) custom-call(bf16[8,256,768]{2,1,0:T(8,128)(2,1)} %x_hbm.1, ...), custom_call_target="tpu_custom_call" | custom-call | flops 86973087744 | bytes 50331648 | tf_op jit(solution)/shard_map/front/pallas_call | solution.py:399
  268.4 0.1 all-reduce.3.cloned.1.call-update
  268.5 272.1 %wide.1 = (bf16[32,256,3072]{2,1,0:T(8,128)(2,1)}, bf16[32,256,3072]{2,1,0:T(8,128)(2,1)}, bf16[32,256,768]{2,1,0:T(8,128)(2,1)}, bf16[8,256,768]{2,1,0:T(8,128)(2,1)}, bf16[8,256,768]{2,1,0:T(8,128)(2,1)}) custom-call(bf16[32,256,768]{2,1,0:T(8,128)(2,1)} %get-tuple-element.16.hall, ...), custom_call_target="tpu_custom_call", output_to_operand_aliasing={{4}: (2, {})} | custom-call | flops 115964116992 | bytes 100663296 | tf_op jit(solution)/shard_map/wide/pallas_call | solution.py:580
  540.6 7.7 %place.1 = (bf16[8,256,768]{2,1,0:T(8,128)(2,1)}, bf16[8,256,768]{2,1,0:T(8,128)(2,1)}) custom-call(bf16[8,256,768]{2,1,0:T(8,128)(2,1)} %get-tuple-element.19.dx, bf16[8,256,768]{2,1,0:T(8,128)(2,1)} %get-tuple-element.20.y), custom_call_target="tpu_custom_call" | custom-call | flops 1572864 | bytes 12582912 | tf_op jit(solution)/shard_map/place/pallas_call | solution.py:636
  548.3 48.2 %gin_low.1 = f32[2,768,3072]{2,1,0:T(8,128)} custom-call(bf16[8192,768]{1,0:T(8,128)(2,1)} %bitcast.26, bf16[8192,3072]{1,0:T(8,128)(2,1)} %bitcast.25), custom_call_target="tpu_custom_call" | custom-call | flops 38654705664 | bytes 72351744 | tf_op jit(solution)/shard_map/gin_low/pallas_call | solution.py:620
  596.6 49.3 %gout_low.1 = f32[2,3072,768]{2,1,0:T(8,128)} custom-call(bf16[8192,3072]{1,0:T(8,128)(2,1)} %bitcast.24, bf16[8192,768]{1,0:T(8,128)(2,1)} %bitcast.27), custom_call_target="tpu_custom_call" | custom-call | flops 38654705664 | bytes 72351744 | tf_op jit(solution)/shard_map/gout_low/pallas_call | solution.py:620
  645.9 0.0 all-reduce.3.cloned.1.call-done
  645.9 0.0 slice-start
  645.9 0.0 slice-start.1
  645.9 0.0 slice-start.2
  645.9 8.8 %constant_dynamic-update-slice_fusion.1 = f32[2,1,768,3072]{3,2,0,1:T(8,128)} fusion(f32[2,1,768,3072]{3,2,0,1:T(8,128)} %bitcast.16, f32[1,1,768,3072]{3,2,0,1:T(8,128)} %get-tuple-element.32), kind=kLoop, calls=%fused_computation.1 | loop fusion | bytes 18874368 | tf_op jit(solution)/shard_map/dynamic_update_slice | solution.py:653
  654.7 0.0 slice-done
  654.7 0.0 slice-done.1
  654.7 0.0 slice-done.2
  654.7 4.4 constant_dynamic-update-slice_fusion
  (1 shorter events, 0.0 us)
Async XLA Ops:
  7.2 638.7 %all-reduce.3.cloned.1.call-start = ((), (), s32[]{:S(2)}) async-start(), calls=%async_computation | async-start | bytes 37748736 | tf_op jit(solution)/shard_map/psum | solution.py:648
  645.9 8.8 %slice-start = ((s8[9437184]{0:T(1024)(128)(4,1)}), s8[4194304]{0:T(1024)(128)(4,1)S(1)}, s32[]{:S(2)}) async-start(s8[9437184]{0:T(1024)(128)(4,1)} %bitcast.12), calls=%async_computation.1 | async-start | bytes 8388608
  645.9 8.8 %slice-start.1 = ((s8[9437184]{0:T(1024)(128)(4,1)}), s8[4194304]{0:T(1024)(128)(4,1)S(1)}, s32[]{:S(2)}) async-start(s8[9437184]{0:T(1024)(128)(4,1)} %bitcast.12), calls=%async_computation.2 | async-start | bytes 8388608
  645.9 8.8 %slice-start.2 = ((s8[9437184]{0:T(1024)(128)(4,1)}), s8[1048576]{0:T(1024)(128)(4,1)S(1)}, s32[]{:S(2)}) async-start(s8[9437184]{0:T(1024)(128)(4,1)} %bitcast.12), calls=%async_computation.3 | async-start | bytes 2097152
Sparse Core Ops, SparseCore 0:
  268.6 322.2 all-reduce.2

commit v4 on v3

--- a/solution.py
+++ b/solution.py
@@ -12,7 +12,7 @@
 ANY = pl.BlockSpec(memory_space=pl.ANY)
 GELU_A = 0.7978845608028654
 GELU_B = 0.044715
-VMEM_LIMIT = 66_000_000
+VMEM_LIMIT = 67_043_328
 
 
 def dot(a, b):
@@ -53,6 +53,14 @@
     lax.fori_loop(lo, hi, body, 0)
 
 
+def head_units(s, micros):
+    return jnp.minimum(jnp.maximum(s - 1, 0), micros)
+
+
+def head_arrivals(s, stages, micros):
+    return jnp.where(s == stages - 1, micros, head_units(s + 1, micros))
+
+
 def signal_all(targets):
     sem = pltpu.get_barrier_semaphore()
     for target in targets:
@@ -71,10 +79,10 @@
         slope[:, cols] = der
 
 
-def front_kernel(stages, levels, micros, chunks, x_hbm, g_hbm, wi_hbm, wo_hbm, hall, y_out, eall, gin_hbm, gout_hbm, aup, qup,
+def front_kernel(stages, levels, micros, chunks, x_hbm, g_hbm, wi_hbm, wo_hbm, hall, y_out, eall, gin_hbm, gout_hbm, aup, qup, alow, qlow, elow,
                  wi, wo, hbuf, obuf, ebuf, gin, gout, abuf, qbuf, slope,
                  w_sem, x_sem, g_sem, f_send, f_recv, b_send, b_recv, y_sem, h_save, h_send, h_recv, e_save, e_send, e_recv,
-                 a_save, a_load, o_sem):
+                 a_save, a_load, o_sem, l_save):
     s = lax.axis_index('stage')
     d = lax.axis_index('data')
     nxt, prv = lax.rem(s + 1, stages), lax.rem(s + stages - 1, stages)
@@ -90,6 +98,7 @@
     inner = jnp.logical_not(last)
     lag = jnp.minimum(3 * (stages - 1 - s), micros)
     defer = s >= stages - 2
+    heads, arrivals = head_units(s, micros), head_arrivals(s, stages, micros)
 
     def w_copies(v):
         return (pltpu.make_async_copy(wi_hbm.at[v], wi.at[v], w_sem.at[v, 0]),
@@ -108,8 +117,19 @@
 
     def b_hop(m, cols=slice(None)):
         return pltpu.make_async_remote_copy(
-            src_ref=obuf.at[m, :, cols], dst_ref=ebuf.at[m, :, cols], send_sem=b_send.at[m], recv_sem=b_recv.at[m],
+            src_ref=obuf.at[lax.rem(m, micros), :, cols], dst_ref=ebuf.at[m, :, cols], send_sem=b_send.at[m], recv_sem=b_recv.at[m],
             device_id={'stage': prv}, device_id_type=MESH)
+
+    def entry(m, cols=slice(None)):
+        return pltpu.make_async_remote_copy(
+            src_ref=obuf.at[m, :, cols], dst_ref=ebuf.at[micros + m, :, cols], send_sem=b_send.at[m], recv_sem=b_recv.at[micros + m],
+            device_id={'stage': prv}, device_id_type=MESH)
+
+    def low_keep(k):
+        return (pltpu.make_async_copy(abuf.at[0], alow.at[k], l_save.at[0]), pltpu.make_async_copy(qbuf.at[0], qlow.at[k], l_save.at[1]))
+
+    def e_low_keep(k):
+        return pltpu.make_async_copy(ebuf.at[micros + k], elow.at[k], l_save.at[2 + k])
 
     def y_copy(m):
         return pltpu.make_async_copy(obuf.at[m], y_out.at[m], y_sem.at[m])
@@ -159,8 +179,7 @@
         return pltpu.make_async_copy(qbuf.at[lax.rem(m, 2)], qup.at[m], a_save.at[1, m])
 
     def loads(m):
-        k = lax.rem(m, 2)
-        return (pltpu.make_async_copy(aup.at[m], abuf.at[k], a_load.at[0, k]), pltpu.make_async_copy(qup.at[m], qbuf.at[k], a_load.at[1, k]))
+        return (pltpu.make_async_copy(aup.at[m], abuf.at[1], a_load.at[0]), pltpu.make_async_copy(qup.at[m], qbuf.at[1], a_load.at[1]))
 
     for v in range(2):
         for c in w_copies(v):
@@ -230,28 +249,38 @@
         def _():
             y_copy(o).start()
 
-    def bwd_unit(m):
-        q = qbuf.at[lax.rem(m, 2)]
-
-        @pl.when(last)
+    def bwd_unit(m, v, slot):
+        q = qbuf.at[slot]
+        upper = m < micros
+        o = lax.rem(m, micros)
+
+        @pl.when(last & upper)
         def _():
             g_copy(m).wait()
             y_copy(m).wait()
 
-        @pl.when(inner)
+        @pl.when(jnp.logical_not(last & upper))
         def _():
             b_hop(m).wait_recv()
+
+        @pl.when(inner & upper)
+        def _():
             f_hop(micros + m, micros + m).wait_send()
 
-        @pl.when(defer & (m >= 2))
+        @pl.when(defer & upper & (m >= 2))
         def _():
             q_keep(m - 2).wait()
 
+        @pl.when(jnp.logical_not(upper))
+        def _():
+            b_hop(o).wait_send()
+            e_low_keep(o).start()
+
         for cols in slices(hid, fb):
-            q[:, cols] = (slope[:, cols] * dot_nt(ebuf[m], wo[1, cols, :])).astype(BF16)
+            q[:, cols] = (slope[:, cols] * dot_nt(ebuf[m], wo[v, cols, :])).astype(BF16)
         for cols in slices(dim, nb):
-            out = ebuf[m, :, cols].astype(F32) + dot_nt(q[...], wi[1, cols, :])
-            obuf[m, :, cols] = out.astype(BF16)
+            out = ebuf[m, :, cols].astype(F32) + dot_nt(q[...], wi[v, cols, :])
+            obuf[o, :, cols] = out.astype(BF16)
 
             @pl.when(jnp.logical_not(first))
             def _():
@@ -259,6 +288,7 @@
 
             @pl.when(first)
             def _():
+                entry(m, cols).start()
                 e_push(m, 0, cols).start()
                 e_push(m, 1, cols).start()
 
@@ -270,9 +300,14 @@
             def _():
                 far(m - 1)
 
-        @pl.when(defer)
+        @pl.when(defer & upper)
         def _():
             q_keep(m).start()
+
+        @pl.when(jnp.logical_not(upper))
+        def _():
+            for c in low_keep(o):
+                c.start()
 
     def far(m):
         for j in range(2):
@@ -280,17 +315,19 @@
         for j in range(2):
             e_forward(m, j).start()
 
-    def weight_unit(m):
-        k = lax.rem(m, 2)
+    def weight_unit(m, k):
         for cols in slices(hid, wb):
             gin[:, cols] += dot_tn(hbuf[micros + m], qbuf[k, :, cols])
             gout[cols, :] += dot_tn(abuf[k, :, cols], ebuf[m])
 
     def step(t):
         m = t - micros - lag
-        active = (m >= 0) & (m < micros)
-        put_off = m - micros
-        w = jnp.where(defer, put_off, m)
+        low = m - micros
+        upper = (m >= 0) & (low < 0)
+        active = (m >= 0) & (low < heads)
+        v = jnp.where(low < 0, 1, 0)
+        slot = jnp.where(low < 0, lax.rem(t + micros + lag, 2), 0)
+        w = jnp.where(defer, low, m)
 
         @pl.when(t == micros)
         def _():
@@ -299,59 +336,62 @@
             for c in w_copies(1):
                 c.wait()
 
-        early = last & active
-
-        @pl.when(early)
-        def _():
-            fwd_wait(t)
-
-        @pl.when(active)
-        def _():
-            @pl.when(defer & (m >= 2))
-            def _():
-                a_keep(m - 2).wait()
-
-            act_pass(hbuf.at[micros + m], wi.at[1], abuf.at[lax.rem(m, 2)], slope, fb)
-
-            @pl.when(defer)
-            def _():
-                a_keep(m).start()
-
-        @pl.when(t < 2 * micros)
-        def _():
-            @pl.when(jnp.logical_not(early))
-            def _():
-                fwd_wait(t)
-
-            fwd_unit(t, jnp.where(early, lax.rem(t + micros, 2), 2))
-
-        @pl.when(active)
-        def _():
-            bwd_unit(m)
-
-        @pl.when(put_off == 0)
+        @pl.when(defer & (low == 0))
         def _():
             for n in range(micros - 2, micros):
                 a_keep(n).wait()
                 q_keep(n).wait()
-            for c in loads(0):
+
+        @pl.when(defer & (low >= 0))
+        def _():
+            for c in loads(low):
                 c.start()
 
-        @pl.when((put_off >= 0) & (put_off < micros - 1))
-        def _():
-            for c in loads(put_off + 1):
-                c.start()
-
-        @pl.when(put_off >= 0)
-        def _():
-            for c in loads(put_off):
+        early = last & upper
+
+        @pl.when(early)
+        def _():
+            fwd_wait(t)
+
+        @pl.when(active)
+        def _():
+            @pl.when(defer & upper & (m >= 2))
+            def _():
+                a_keep(m - 2).wait()
+
+            @pl.when(low >= 1)
+            def _():
+                for c in low_keep(low - 1):
+                    c.wait()
+
+            act_pass(hbuf.at[jnp.where(low < 0, micros + m, low)], wi.at[v], abuf.at[slot], slope, fb)
+
+            @pl.when(defer & upper)
+            def _():
+                a_keep(m).start()
+
+        @pl.when(t < 2 * micros)
+        def _():
+            @pl.when(jnp.logical_not(early))
+            def _():
+                fwd_wait(t)
+
+            fwd_unit(t, jnp.where(early, slot, 2))
+
+        @pl.when(active)
+        def _():
+            bwd_unit(m, v, slot)
+
+        @pl.when(defer & (low >= 0))
+        def _():
+            for c in loads(low):
                 c.wait()
 
         @pl.when((w >= 0) & (w < micros))
         def _():
-            weight_unit(w)
-
-    loop(0, 2 * micros + lag + jnp.where(defer, micros, 0), step)
+            weight_unit(w, jnp.where(defer, 1, slot))
+
+    loop(0, 2 * micros + lag + jnp.where(defer, micros, heads), step)
 
     outs = (pltpu.make_async_copy(gin, gin_hbm, o_sem.at[0]), pltpu.make_async_copy(gout, gout_hbm, o_sem.at[1]))
     for c in outs:
@@ -369,12 +409,26 @@
         h_forward(m, 1).wait_send()
         h_whole(m).wait_recv()
 
-        @pl.when(jnp.logical_not(first))
+        @pl.when(jnp.logical_not(first) & (m >= heads))
         def _():
             b_hop(m).wait_send()
 
+        @pl.when(m < heads)
+        def _():
+            b_hop(micros + m).wait_send()
+
+        @pl.when((m >= heads) & (m < arrivals))
+        def _():
+            b_hop(micros + m).wait_recv()
+            e_low_keep(m).start()
+
+        @pl.when(m < arrivals)
+        def _():
+            e_low_keep(m).wait()
+
         @pl.when(first)
         def _():
+            entry(m).wait_send()
             e_keep(m).wait()
             for j in range(2):
                 e_push(m, j).wait_send()
@@ -382,6 +436,12 @@
             e_whole(m).wait_recv()
 
     loop(0, micros, drain)
+
+    @pl.when(heads > 0)
+    def _():
+        for c in low_keep(heads - 1):
+            c.wait()
+
     for c in outs:
         c.wait()
 
@@ -395,19 +455,22 @@
     def rows(n):
         return jax.ShapeDtypeStruct((n * micros, tokens, dim), BF16)
 
-    acts = jax.ShapeDtypeStruct((micros, tokens, hid), BF16)
+    def acts(n):
+        return jax.ShapeDtypeStruct((n * micros, tokens, hid), BF16)
+
     return pl.pallas_call(
         functools.partial(front_kernel, stages, levels, micros, chunks),
-        out_shape=(rows(4), rows(1), rows(4), jax.ShapeDtypeStruct((dim, hid), F32), jax.ShapeDtypeStruct((hid, dim), F32), acts, acts),
-        in_specs=[ANY] * 4, out_specs=(ANY,) * 7,
+        out_shape=(rows(4), rows(1), rows(4), jax.ShapeDtypeStruct((dim, hid), F32), jax.ShapeDtypeStruct((hid, dim), F32),
+                   acts(1), acts(1), acts(levels), acts(levels), rows(levels)),
+        in_specs=[ANY] * 4, out_specs=(ANY,) * 10,
         scratch_shapes=[
             pltpu.VMEM((2, dim, hid), BF16), pltpu.VMEM((2, hid, dim), BF16),
-            pltpu.VMEM((2 * micros, tokens, dim), BF16), pltpu.VMEM((micros, tokens, dim), BF16), pltpu.VMEM((micros, tokens, dim), BF16),
+            pltpu.VMEM((2 * micros, tokens, dim), BF16), pltpu.VMEM((micros, tokens, dim), BF16), pltpu.VMEM((2 * micros, tokens, dim), BF16),
             pltpu.VMEM((dim, hid), F32), pltpu.VMEM((hid, dim), F32),
             pltpu.VMEM((3, tokens, hid), BF16), pltpu.VMEM((2, tokens, hid), BF16), pltpu.VMEM((tokens, hid), F32),
-            dma((2, 2)), dma((micros,)), dma((micros,)), dma((2 * micros,)), dma((2 * micros,)), dma((micros,)), dma((micros,)), dma((micros,)),
+            dma((2, 2)), dma((micros,)), dma((micros,)), dma((2 * micros,)), dma((2 * micros,)), dma((2 * micros,)), dma((2 * micros,)), dma((micros,)),
             dma((micros,)), dma((4, micros)), dma((3, micros)), dma((micros,)), dma((4, micros)), dma((3, micros)),
-            dma((2, micros)), dma((2, 2)), dma((2,)),
+            dma((2, micros)), dma((2,)), dma((2,)), dma((2 + micros,)),
         ],
         compiler_params=pltpu.CompilerParams(collective_id=0, has_side_effects=True, vmem_limit_bytes=VMEM_LIMIT),
         cost_estimate=pl.CostEstimate(flops=micros * 18 * tokens * dim * hid, bytes_accessed=4 * micros * tokens * hid * 2,
@@ -416,9 +479,9 @@
     )(x, g, w_in, w_out)
 
 
-def wide_kernel(stages, micros, chunks, hall, eall, _, wi_hbm, wo_hbm, a_out, q_out, e_out, dx_out, y_out,
+def wide_kernel(stages, micros, chunks, hall, eall, _y, _a, _q, _e, wi_hbm, wo_hbm, a_out, q_out, e_out, dx_out, y_out,
                 wi, wo, hbuf, obuf, ebuf, abuf, qbuf,
-                w_sem, h_sem, n_send, b_send, b_recv, dx_sem, dx_send, dx_recv, y_send, y_recv, s_sem):
+                w_sem, h_sem, n_send, b_send, b_recv, dx_sem, dx_send, dx_recv, y_send, y_recv, s_sem, l_sem):
     s = lax.axis_index('stage')
     nxt, prv = lax.rem(s + 1, stages), lax.rem(s + stages - 1, stages)
     dim, hid = wi.shape
@@ -428,6 +491,7 @@
     hslots = hbuf.shape[0]
     first = s == 0
     last = s == stages - 1
+    heads, arrivals = head_units(s, micros), head_arrivals(s, stages, micros)
 
     w_copies = (pltpu.make_async_copy(wi_hbm.at[0], wi, w_sem.at[0]), pltpu.make_async_copy(wo_hbm.at[0], wo, w_sem.at[1]))
 
@@ -458,9 +522,12 @@
             src_ref=y_out.at[m], dst_ref=y_out.at[m], send_sem=y_send.at[m], recv_sem=y_recv.at[m],
             device_id={'stage': nxt}, device_id_type=MESH)
 
+    def e_load(i):
+        return pltpu.make_async_copy(e_out.at[i], ebuf.at[i], l_sem.at[i])
+
     def relay(i):
-        my = jnp.where(last, i - 1, i - 2 - 3 * s)
-        mx = i - 1 - 3 * s
+        my = jnp.where(last, i, i - 2 - 2 * s)
+        mx = i - 1 - 2 * s
 
         @pl.when((my >= 0) & (my < micros))
         def _():
@@ -488,13 +555,14 @@
     for c in w_copies:
         c.start()
     for i in range(hslots - 1):
-        h_copy(i).start()
+        h_copy(heads + i).start()
+    loop(heads, arrivals, lambda i: e_load(i).start())
 
     signal_all([{'stage': lax.rem(s + step, stages)} for step in range(1, stages)])
 
     @pl.when(first)
     def _():
-        loop(0, units, lambda i: entry(i).start())
+        loop(micros, units, lambda i: entry(i).start())
 
     for c in w_copies:
         c.wait()
@@ -509,16 +577,23 @@
             h_copy(i + hslots - 1).start()
 
         h_copy(i).wait()
-        b_hop(i).wait_recv()
-
-        @pl.when(i >= 2)
+
+        @pl.when(i < arrivals)
+        def _():
+            e_load(i).wait()
+
+        @pl.when(i >= arrivals)
+        def _():
+            b_hop(i).wait_recv()
+
+        @pl.when(i >= heads + 2)
         def _():
             for c in keep(i - 2):
                 c.wait()
 
-        relay(i)
-
-        @pl.when(jnp.logical_not(first) & (i >= micros))
+        relay(i - heads)
+
+        @pl.when(jnp.logical_not(first) & (i >= heads + micros))
         def _():
             b_hop(i - micros).wait_send()
 
@@ -545,12 +620,12 @@
         for c in keep(i):
             c.start()
 
-    loop(0, units, unit)
-    loop(units, max(units, micros + 3 * stages - 2), relay)
+    loop(heads, units, unit)
+    loop(units - heads, jnp.maximum(units - heads, micros + 2 * stages - 1), relay)
 
     @pl.when(first)
     def _():
-        loop(0, units, lambda i: entry(i).wait_send())
+        loop(micros, units, lambda i: entry(i).wait_send())
         loop(0, micros, lambda m: dx_copy(m).wait())
 
     @pl.when(jnp.logical_not(first))
@@ -570,7 +645,7 @@
             c.wait()
 
 
-def run_wide(stages, micros, hall, eall, y, w_in, w_out):
+def run_wide(stages, micros, hall, eall, y, alow, qlow, elow, w_in, w_out):
     units, tokens, dim = hall.shape
     _, _, hid = w_in.shape
     chunks = 3 if dim % 384 == 0 else 1
@@ -580,20 +655,20 @@
     return pl.pallas_call(
         functools.partial(wide_kernel, stages, micros, chunks),
         out_shape=(acts, acts, jax.ShapeDtypeStruct((units, tokens, dim), BF16), small, small),
-        in_specs=[ANY] * 5, out_specs=(ANY,) * 5,
+        in_specs=[ANY] * 8, out_specs=(ANY,) * 5,
         scratch_shapes=[
             pltpu.VMEM((dim, hid), BF16), pltpu.VMEM((hid, dim), BF16),
             pltpu.VMEM((4, tokens, dim), BF16), pltpu.VMEM((micros, tokens, dim), BF16), pltpu.VMEM((units, tokens, dim), BF16),
             pltpu.VMEM((2, tokens, hid), BF16), pltpu.VMEM((2, tokens, hid), BF16),
             dma((2,)), dma((4,)), dma((units,)), dma((micros,)), dma((units,)), dma((micros,)), dma((micros,)), dma((micros,)),
-            dma((micros,)), dma((micros,)), dma((3, 2)),
+            dma((micros,)), dma((micros,)), dma((3, 2)), dma((micros,)),
         ],
-        input_output_aliases={2: 4},
+        input_output_aliases={2: 4, 3: 0, 4: 1, 5: 2},
         compiler_params=pltpu.CompilerParams(collective_id=1, has_side_effects=True, vmem_limit_bytes=VMEM_LIMIT),
         cost_estimate=pl.CostEstimate(flops=units * 6 * tokens * dim * hid, bytes_accessed=units * tokens * hid * 4,
                                       transcendentals=units * tokens * hid),
         name='wide',
-    )(hall, eall, y, w_in, w_out)
+    )(hall, eall, y, alow, qlow, elow, w_in, w_out)
 
 
 def wgrad_kernel(lhs, rhs, out):
@@ -644,9 +719,9 @@
 
     def local_fn(x, g, w_in, w_out):
         wi, wo = w_in[:, 0], w_out[:, 0]
-        hall, y, eall, gin_up, gout_up, _, _ = run_front(stages, levels, x, g, wi, wo)
+        hall, y, eall, gin_up, gout_up, _, _, alow, qlow, elow = run_front(stages, levels, x, g, wi, wo)
         gin_up, gout_up = lax.psum((gin_up, gout_up), 'data')
-        alow, qlow, elow, dx, y = run_wide(stages, x.shape[0], hall, eall, y, wi, wo)
+        alow, qlow, elow, dx, y = run_wide(stages, x.shape[0], hall, eall, y, alow, qlow, elow, wi, wo)
         grad_in = run_wgrad(hall, qlow, False, 'gin_low')
         grad_out = run_wgrad(alow, elow, True, 'gout_low')
         dx, y = run_place(dx, y)

time: 666 us -> 637 us (0.956)
  Pallas kernels: 639 us -> 610 us
    pallas_call x1, Pallas kernels: 272 us -> 243 us  [run_wide(): pl.pallas_call(functools.partial(wide_kernel, stages, micros, chunks), ou...]
  transfers between devices with their start and end apart: 1 -> 1, of which waited for: 0 -> 0; matrix products, arithmetic and copies ran while one was open for 0% -> 0% of each run, Pallas kernels for 57% -> 55%
where the time goes in v4:
time: 637 us
  Pallas kernels  610 us (96%)
  between operations  14.1 us (2%)
  local copies, waits for them, and re-layouts  13.1 us (2%)
    pallas_call x1, Pallas kernels, run_front(): pl.pallas_call(functools.partial(front_kernel, stages, levels, micros, ch...  261 us
    pallas_call x1, Pallas kernels, run_wide(): pl.pallas_call(functools.partial(wide_kernel, stages, micros, chunks), ou...  243 us
    pallas_call x2, Pallas kernels, run_wgrad(): pl.pallas_call(wgrad_kernel, grid=grid, out_shape=jax.ShapeDtypeStruct((2...  97.6 us
  transfers between devices with their start and end apart: 1, of which 0 were waited for; matrix products, arithmetic and copies ran while one was open for 0% of the time, Pallas kernels for 55%

profile of v4, /device:TPU:96, one launch (start us, length us, event | category | flops | bytes accessed | tf_op | source)
XLA Modules:
  0.0 637.1 jit_solution(15884616380982524962)
XLA Ops:
  7.2 0.1 all-reduce.3.cloned.1.call-start
  7.2 261.5 %front.1 = (bf16[32,256,768]{2,1,0:T(8,128)(2,1)}, bf16[8,256,768]{2,1,0:T(8,128)(2,1)}, bf16[32,256,768]{2,1,0:T(8,128)(2,1)}, f32[768,3072]{1,0:T(8,128)}, f32...) custom-call(bf16[8,256,768]{2,1,0:T(8,128)(2,1)} %x_hbm.1, ...), custom_call_target="tpu_custom_call" | custom-call | flops 86973087744 | bytes 50331648 | tf_op jit(solution)/shard_map/front/pallas_call | solution.py:461
  268.7 0.1 all-reduce.3.cloned.1.call-update
  268.8 242.9 %wide.1 = (bf16[32,256,3072]{2,1,0:T(8,128)(2,1)}, bf16[32,256,3072]{2,1,0:T(8,128)(2,1)}, bf16[32,256,768]{2,1,0:T(8,128)(2,1)}, bf16[8,256,768]{2,1,0:T(8,128)(2,1)}, bf16[8,256,768]{2,1,0:T(8,128)(2,1)}) custom-call(bf16[32,256,768]{2,1,0:T(8,128)(2,1)} %get-tuple-element.19.hall, ...), custom_call_target="tpu_custom_call", output_to_operand_aliasing={{4}: (2, {}), {0}: (3, {}), {1}: (4, {}), {2}: (5, {})} | custom-call | flops 115964116992 | bytes 100663296 | tf_op jit(solution)/shard_map/wide/pallas_call | solution.py:655
  511.8 7.7 %place.1 = (bf16[8,256,768]{2,1,0:T(8,128)(2,1)}, bf16[8,256,768]{2,1,0:T(8,128)(2,1)}) custom-call(bf16[8,256,768]{2,1,0:T(8,128)(2,1)} %get-tuple-element.25.dx, bf16[8,256,768]{2,1,0:T(8,128)(2,1)} %get-tuple-element.26.y), custom_call_target="tpu_custom_call" | custom-call | flops 1572864 | bytes 12582912 | tf_op jit(solution)/shard_map/place/pallas_call | solution.py:711
  519.5 48.2 %gin_low.1 = f32[2,768,3072]{2,1,0:T(8,128)} custom-call(bf16[8192,768]{1,0:T(8,128)(2,1)} %bitcast.26, bf16[8192,3072]{1,0:T(8,128)(2,1)} %bitcast.25), custom_call_target="tpu_custom_call" | custom-call | flops 38654705664 | bytes 72351744 | tf_op jit(solution)/shard_map/gin_low/pallas_call | solution.py:695
  567.7 49.3 %gout_low.1 = f32[2,3072,768]{2,1,0:T(8,128)} custom-call(bf16[8192,3072]{1,0:T(8,128)(2,1)} %bitcast.24, bf16[8192,768]{1,0:T(8,128)(2,1)} %bitcast.27), custom_call_target="tpu_custom_call" | custom-call | flops 38654705664 | bytes 72351744 | tf_op jit(solution)/shard_map/gout_low/pallas_call | solution.py:695
  617.1 0.0 all-reduce.3.cloned.1.call-done
  617.1 0.0 slice-start
  617.1 0.0 slice-start.1
  617.1 0.0 slice-start.2
  617.1 8.8 %constant_dynamic-update-slice_fusion.1 = f32[2,1,768,3072]{3,2,0,1:T(8,128)} fusion(f32[2,1,768,3072]{3,2,0,1:T(8,128)} %bitcast.16, f32[1,1,768,3072]{3,2,0,1:T(8,128)} %get-tuple-element.38), kind=kLoop, calls=%fused_computation.1 | loop fusion | bytes 18874368 | tf_op jit(solution)/shard_map/dynamic_update_slice | solution.py:728
  625.8 0.0 slice-done
  625.8 0.0 slice-done.1
  625.8 0.0 slice-done.2
  625.9 4.4 constant_dynamic-update-slice_fusion
  (1 shorter events, 0.0 us)
Async XLA Ops:
  7.2 609.9 %all-reduce.3.cloned.1.call-start = ((), (), s32[]{:S(2)}) async-start(), calls=%async_computation | async-start | bytes 37748736 | tf_op jit(solution)/shard_map/psum | solution.py:723
  617.1 8.8 %slice-start = ((s8[9437184]{0:T(1024)(128)(4,1)}), s8[4194304]{0:T(1024)(128)(4,1)S(1)}, s32[]{:S(2)}) async-start(s8[9437184]{0:T(1024)(128)(4,1)} %bitcast.12), calls=%async_computation.1 | async-start | bytes 8388608
  617.1 8.8 %slice-start.1 = ((s8[9437184]{0:T(1024)(128)(4,1)}), s8[4194304]{0:T(1024)(128)(4,1)S(1)}, s32[]{:S(2)}) async-start(s8[9437184]{0:T(1024)(128)(4,1)} %bitcast.12), calls=%async_computation.2 | async-start | bytes 8388608
  617.1 8.8 %slice-start.2 = ((s8[9437184]{0:T(1024)(128)(4,1)}), s8[1048576]{0:T(1024)(128)(4,1)S(1)}, s32[]{:S(2)}) async-start(s8[9437184]{0:T(1024)(128)(4,1)} %bitcast.12), calls=%async_computation.3 | async-start | bytes 2097152
Sparse Core Ops, SparseCore 0:
  268.9 333.2 all-reduce.2

commit v5 on v4

--- a/solution.py
+++ b/solution.py
@@ -54,7 +54,7 @@
 
 
 def head_units(s, micros):
-    return jnp.minimum(jnp.maximum(s - 1, 0), micros)
+    return jnp.minimum(jnp.maximum(s - 1, 0), micros // 2)
 
 
 def head_arrivals(s, stages, micros):
@@ -79,7 +79,7 @@
         slope[:, cols] = der
 
 
-def front_kernel(stages, levels, micros, chunks, x_hbm, g_hbm, wi_hbm, wo_hbm, hall, y_out, eall, gin_hbm, gout_hbm, aup, qup, alow, qlow, elow,
+def front_kernel(stages, levels, micros, chunks, x_hbm, g_hbm, wi_hbm, wo_hbm, hall, y_out, eall, gin_hbm, gout_hbm, aup, qup, aqlow, elow,
                  wi, wo, hbuf, obuf, ebuf, gin, gout, abuf, qbuf, slope,
                  w_sem, x_sem, g_sem, f_send, f_recv, b_send, b_recv, y_sem, h_save, h_send, h_recv, e_save, e_send, e_recv,
                  a_save, a_load, o_sem, l_save):
@@ -126,7 +126,7 @@
             device_id={'stage': prv}, device_id_type=MESH)
 
     def low_keep(k):
-        return (pltpu.make_async_copy(abuf.at[0], alow.at[k], l_save.at[0]), pltpu.make_async_copy(qbuf.at[0], qlow.at[k], l_save.at[1]))
+        return (pltpu.make_async_copy(abuf.at[0], aqlow.at[k, 0], l_save.at[0]), pltpu.make_async_copy(qbuf.at[0], aqlow.at[k, 1], l_save.at[1]))
 
     def e_low_keep(k):
         return pltpu.make_async_copy(ebuf.at[micros + k], elow.at[k], l_save.at[2 + k])
@@ -166,6 +166,11 @@
         return pltpu.make_async_remote_copy(
             src_ref=eall.at[(2 - j) * micros + m, rows], dst_ref=eall.at[3 * micros + m, rows], send_sem=e_send.at[2 + j, m],
             recv_sem=e_recv.at[2, m], device_id={'data': (up, down)[j]}, device_id_type=MESH)
+
+    def e_direct(m):
+        return pltpu.make_async_remote_copy(
+            src_ref=obuf.at[m], dst_ref=eall.at[3 * micros + m], send_sem=e_send.at[2, m], recv_sem=e_recv.at[2, m],
+            device_id={'data': lax.rem(d + 2, levels)}, device_id_type=MESH)
 
     def e_whole(m):
         return pltpu.make_async_remote_copy(
@@ -193,7 +198,7 @@
     def _():
         loop(0, micros, lambda m: g_copy(m).start())
 
-    signal_all([{'stage': lax.rem(s + step, stages)} for step in range(1, stages)] + [{'data': up}, {'data': down}])
+    signal_all([{'stage': lax.rem(s + step, stages)} for step in range(1, stages)] + [{'data': up}, {'data': down}, {'data': lax.rem(d + 2, levels)}])
 
     for c in w_copies(0):
         c.wait()
@@ -300,6 +305,10 @@
             def _():
                 far(m - 1)
 
+            @pl.when(m == micros - 1)
+            def _():
+                e_direct(m).start()
+
         @pl.when(defer & upper)
         def _():
             q_keep(m).start()
@@ -397,10 +406,6 @@
     for c in outs:
         c.start()
 
-    @pl.when(first)
-    def _():
-        far(micros - 1)
-
     def drain(m):
         h_keep(m).wait()
         h_push(m, 0).wait_send()
@@ -432,8 +437,18 @@
             e_keep(m).wait()
             for j in range(2):
                 e_push(m, j).wait_send()
-                e_forward(m, j).wait_send()
             e_whole(m).wait_recv()
+
+            @pl.when(m < micros - 1)
+            def _():
+                for j in range(2):
+                    e_forward(m, j).wait_send()
+
+            @pl.when(m == micros - 1)
+            def _():
+                e_direct(m).wait_send()
+                for j in range(2):
+                    e_push(m, j).wait_recv()
 
     loop(0, micros, drain)
 
@@ -461,8 +476,8 @@
     return pl.pallas_call(
         functools.partial(front_kernel, stages, levels, micros, chunks),
         out_shape=(rows(4), rows(1), rows(4), jax.ShapeDtypeStruct((dim, hid), F32), jax.ShapeDtypeStruct((hid, dim), F32),
-                   acts(1), acts(1), acts(levels), acts(levels), rows(levels)),
-        in_specs=[ANY] * 4, out_specs=(ANY,) * 10,
+                   acts(1), acts(1), jax.ShapeDtypeStruct((levels * micros, 2, tokens, hid), BF16), rows(levels)),
+        in_specs=[ANY] * 4, out_specs=(ANY,) * 9,
         scratch_shapes=[
             pltpu.VMEM((2, dim, hid), BF16), pltpu.VMEM((2, hid, dim), BF16),
             pltpu.VMEM((2 * micros, tokens, dim), BF16), pltpu.VMEM((micros, tokens, dim), BF16), pltpu.VMEM((2 * micros, tokens, dim), BF16),
@@ -479,34 +494,43 @@
     )(x, g, w_in, w_out)
 
 
-def wide_kernel(stages, micros, chunks, hall, eall, _y, _a, _q, _e, wi_hbm, wo_hbm, a_out, q_out, e_out, dx_out, y_out,
-                wi, wo, hbuf, obuf, ebuf, abuf, qbuf,
-                w_sem, h_sem, n_send, b_send, b_recv, dx_sem, dx_send, dx_recv, y_send, y_recv, s_sem, l_sem):
+def wide_kernel(stages, micros, hall, eall, _y, _aq, _e, wi_hbm, wo_hbm, aq_out, e_out, dx_out, y_out,
+                wi, wo, hbuf, obuf, ebuf, aqbuf,
+                w_sem, h_sem, n_send, b_send, b_recv, dx_sem, dx_send, dx_recv, y_send, y_recv, s_sem, k_sem, l_sem):
     s = lax.axis_index('stage')
     nxt, prv = lax.rem(s + 1, stages), lax.rem(s + stages - 1, stages)
     dim, hid = wi.shape
     units = ebuf.shape[0]
-    nb = dim // chunks
     fb = pick_block(hid, 768)
-    hslots = hbuf.shape[0]
+    ob = pick_block(dim, 256)
+    groups = units // micros
     first = s == 0
     last = s == stages - 1
     heads, arrivals = head_units(s, micros), head_arrivals(s, stages, micros)
 
     w_copies = (pltpu.make_async_copy(wi_hbm.at[0], wi, w_sem.at[0]), pltpu.make_async_copy(wo_hbm.at[0], wo, w_sem.at[1]))
 
-    def h_copy(i):
-        return pltpu.make_async_copy(hall.at[i], hbuf.at[lax.rem(i, hslots)], h_sem.at[lax.rem(i, hslots)])
+    def part(k):
+        return pl.ds(k * micros, micros)
+
+    def h_copy(k):
+        return pltpu.make_async_copy(hall.at[part(k)], hbuf.at[part(k)], h_sem.at[k])
+
+    def e_part(k):
+        return pltpu.make_async_copy(ebuf.at[part(k)], e_out.at[part(k)], k_sem.at[k])
+
+    def e_keep(i):
+        return pltpu.make_async_copy(ebuf.at[i], e_out.at[i], l_sem.at[i])
 
     def entry(i):
         return pltpu.make_async_remote_copy(
             src_ref=eall.at[i], dst_ref=ebuf.at[i], send_sem=n_send.at[i], recv_sem=b_recv.at[i],
             device_id={'stage': prv}, device_id_type=MESH)
 
-    def b_hop(i, cols=slice(None)):
+    def b_hop(i):
         o = lax.rem(i, micros)
         return pltpu.make_async_remote_copy(
-            src_ref=obuf.at[o, :, cols], dst_ref=ebuf.at[i, :, cols], send_sem=b_send.at[o], recv_sem=b_recv.at[i],
+            src_ref=obuf.at[o], dst_ref=ebuf.at[i], send_sem=b_send.at[o], recv_sem=b_recv.at[i],
             device_id={'stage': prv}, device_id_type=MESH)
 
     def dx_copy(m):
@@ -549,13 +573,12 @@
 
     def keep(i):
         k = lax.rem(i, 2)
-        return (pltpu.make_async_copy(abuf.at[k], a_out.at[i], s_sem.at[0, k]), pltpu.make_async_copy(qbuf.at[k], q_out.at[i], s_sem.at[1, k]),
-                pltpu.make_async_copy(ebuf.at[i], e_out.at[i], s_sem.at[2, k]))
+        return pltpu.make_async_copy(aqbuf.at[k], aq_out.at[i], s_sem.at[k])
 
     for c in w_copies:
         c.start()
-    for i in range(hslots - 1):
-        h_copy(heads + i).start()
+    for k in range(groups):
+        h_copy(k).start()
     loop(heads, arrivals, lambda i: e_load(i).start())
 
     signal_all([{'stage': lax.rem(s + step, stages)} for step in range(1, stages)])
@@ -569,14 +592,12 @@
 
     def unit(i):
         k = lax.rem(i, 2)
-        a, q, h = abuf.at[k], qbuf.at[k], hbuf.at[lax.rem(i, hslots)]
+        a, q = aqbuf.at[k, 0], aqbuf.at[k, 1]
         o = lax.rem(i, micros)
 
-        @pl.when(i + hslots - 1 < units)
-        def _():
-            h_copy(i + hslots - 1).start()
-
-        h_copy(i).wait()
+        @pl.when((o == 0) | (i == heads))
+        def _():
+            h_copy(i // micros).wait()
 
         @pl.when(i < arrivals)
         def _():
@@ -588,37 +609,43 @@
 
         @pl.when(i >= heads + 2)
         def _():
-            for c in keep(i - 2):
-                c.wait()
+            keep(i - 2).wait()
 
         relay(i - heads)
 
-        @pl.when(jnp.logical_not(first) & (i >= heads + micros))
-        def _():
-            b_hop(i - micros).wait_send()
-
         for cols in slices(hid, fb):
-            act, der = gelu_and_slope(dot(h[...], wi[:, cols]))
+            act, der = gelu_and_slope(dot(hbuf[i], wi[:, cols]))
             a[:, cols] = act.astype(BF16)
             q[:, cols] = (der * dot_nt(ebuf[i], wo[cols, :])).astype(BF16)
 
+        keep(i).start()
+
+        @pl.when(jnp.logical_not(first) & (i >= heads + micros))
+        def _():
+            b_hop(i - micros).wait_send()
+
         @pl.when(jnp.logical_not(first) | (i < micros))
         def _():
-            for cols in slices(dim, nb):
+            for cols in slices(dim, ob):
                 out = ebuf[i, :, cols].astype(F32) + dot_nt(q[...], wi[cols, :])
                 obuf[o, :, cols] = out.astype(BF16)
 
-                @pl.when(jnp.logical_not(first))
-                def _():
-                    b_hop(i, cols).start()
+            @pl.when(jnp.logical_not(first))
+            def _():
+                b_hop(i).start()
 
         @pl.when(first & (i < micros))
         def _():
             dx_copy(i).start()
             dx_hop(i, obuf).start()
 
-        for c in keep(i):
-            c.start()
+        @pl.when((i >= arrivals) & (i < micros))
+        def _():
+            e_keep(i).start()
+
+        @pl.when((o == micros - 1) & (i >= micros))
+        def _():
+            e_part(i // micros).start()
 
     loop(heads, units, unit)
     loop(units - heads, jnp.maximum(units - heads, micros + 2 * stages - 1), relay)
@@ -641,77 +668,82 @@
         loop(0, micros, lambda m: y_hop(m).wait_send())
 
     for i in (units - 2, units - 1):
-        for c in keep(i):
-            c.wait()
-
-
-def run_wide(stages, micros, hall, eall, y, alow, qlow, elow, w_in, w_out):
+        keep(i).wait()
+    loop(arrivals, micros, lambda i: e_keep(i).wait())
+    for k in range(1, groups):
+        e_part(k).wait()
+
+
+def run_wide(stages, micros, hall, eall, y, aqlow, elow, w_in, w_out):
     units, tokens, dim = hall.shape
     _, _, hid = w_in.shape
-    chunks = 3 if dim % 384 == 0 else 1
+    groups = units // micros
     dma = pltpu.SemaphoreType.DMA
     small = jax.ShapeDtypeStruct((micros, tokens, dim), BF16)
-    acts = jax.ShapeDtypeStruct((units, tokens, hid), BF16)
+    acts = jax.ShapeDtypeStruct((units, 2, tokens, hid), BF16)
     return pl.pallas_call(
-        functools.partial(wide_kernel, stages, micros, chunks),
-        out_shape=(acts, acts, jax.ShapeDtypeStruct((units, tokens, dim), BF16), small, small),
-        in_specs=[ANY] * 8, out_specs=(ANY,) * 5,
+        functools.partial(wide_kernel, stages, micros),
+        out_shape=(acts, jax.ShapeDtypeStruct((units, tokens, dim), BF16), small, small),
+        in_specs=[ANY] * 7, out_specs=(ANY,) * 4,
         scratch_shapes=[
             pltpu.VMEM((dim, hid), BF16), pltpu.VMEM((hid, dim), BF16),
-            pltpu.VMEM((4, tokens, dim), BF16), pltpu.VMEM((micros, tokens, dim), BF16), pltpu.VMEM((units, tokens, dim), BF16),
-            pltpu.VMEM((2, tokens, hid), BF16), pltpu.VMEM((2, tokens, hid), BF16),
-            dma((2,)), dma((4,)), dma((units,)), dma((micros,)), dma((units,)), dma((micros,)), dma((micros,)), dma((micros,)),
-            dma((micros,)), dma((micros,)), dma((3, 2)), dma((micros,)),
+            pltpu.VMEM((units, tokens, dim), BF16), pltpu.VMEM((micros, tokens, dim), BF16), pltpu.VMEM((units, tokens, dim), BF16),
+            pltpu.VMEM((2, 2, tokens, hid), BF16),
+            dma((2,)), dma((groups,)), dma((units,)), dma((micros,)), dma((units,)), dma((micros,)), dma((micros,)), dma((micros,)),
+            dma((micros,)), dma((micros,)), dma((2,)), dma((groups,)), dma((micros,)),
         ],
-        input_output_aliases={2: 4, 3: 0, 4: 1, 5: 2},
+        input_output_aliases={2: 3, 3: 0, 4: 1},
         compiler_params=pltpu.CompilerParams(collective_id=1, has_side_effects=True, vmem_limit_bytes=VMEM_LIMIT),
         cost_estimate=pl.CostEstimate(flops=units * 6 * tokens * dim * hid, bytes_accessed=units * tokens * hid * 4,
                                       transcendentals=units * tokens * hid),
         name='wide',
-    )(hall, eall, y, alow, qlow, elow, w_in, w_out)
-
-
-def wgrad_kernel(lhs, rhs, out):
+    )(hall, eall, y, aqlow, elow, w_in, w_out)
+
+
+def wgrad_kernel(lhs, rhs, *refs):
+    others = (len(refs) - 1) // 2
+    out = refs[others]
+
     @pl.when(pl.program_id(1) == 0)
     def _():
         out[...] = jnp.zeros_like(out)
 
-    out[0] += dot_tn(lhs[...], rhs[...])
-
-
-def run_wgrad(lhs, rhs, split_lhs, name):
-    lhs, rhs = lhs.reshape(-1, lhs.shape[-1]), rhs.reshape(-1, rhs.shape[-1])
-    tokens, m, n = lhs.shape[0], lhs.shape[1], rhs.shape[1]
-    kb = pick_block(tokens, 2048)
-    fb = pick_block(m if split_lhs else n, 1024)
+    for src, dst in zip(refs[:others], refs[others + 1:]):
+        dst[...] = src[...]
+    lhs, rhs = (ref[...].reshape(-1, ref.shape[-1]) for ref in (lhs, rhs))
+    out[0] += dot_tn(lhs, rhs)
+
+
+def run_wgrad(rows, aq, which, split_lhs, others, name):
+    units, tokens, dim = rows.shape
+    hid = aq.shape[-1]
+    ub = pick_block(units, max(1, 2048 // tokens))
+    fb = pick_block(hid, 1024)
+    grid = (hid // fb, units // ub)
+    rows_spec = pl.BlockSpec((ub, tokens, dim), lambda j, k: (k, 0, 0))
+    aq_spec = pl.BlockSpec((ub, None, tokens, fb), lambda j, k: (k, which, 0, j))
     if split_lhs:
-        grid, block = (m // fb, tokens // kb), (1, fb, n)
-        lhs_spec, rhs_spec = pl.BlockSpec((kb, fb), lambda j, k: (k, j)), pl.BlockSpec((kb, n), lambda j, k: (k, 0))
-        place = lambda j, k: (0, j, 0)
+        operands, specs = [aq, rows], [aq_spec, rows_spec]
+        shape, out_spec = (2, hid, dim), pl.BlockSpec((1, fb, dim), lambda j, k: (0, j, 0))
     else:
-        grid, block = (n // fb, tokens // kb), (1, m, fb)
-        lhs_spec, rhs_spec = pl.BlockSpec((kb, m), lambda j, k: (k, 0)), pl.BlockSpec((kb, fb), lambda j, k: (k, j))
-        place = lambda j, k: (0, 0, j)
+        operands, specs = [rows, aq], [rows_spec, aq_spec]
+        shape, out_spec = (2, dim, hid), pl.BlockSpec((1, dim, fb), lambda j, k: (0, 0, j))
+    out_shapes, out_specs = [jax.ShapeDtypeStruct(shape, F32)], [out_spec]
+    for other in others:
+        count = pick_block(other.shape[0], grid[0] * grid[1])
+        spec = pl.BlockSpec((other.shape[0] // count,) + other.shape[1:],
+                            lambda j, k, count=count: (jnp.minimum(j * grid[1] + k, count - 1), 0, 0))
+        operands.append(other)
+        specs.append(spec)
+        out_shapes.append(jax.ShapeDtypeStruct(other.shape, other.dtype))
+        out_specs.append(spec)
     return pl.pallas_call(
-        wgrad_kernel, grid=grid, out_shape=jax.ShapeDtypeStruct((2, m, n), F32), in_specs=[lhs_spec, rhs_spec],
-        out_specs=pl.BlockSpec(block, place), compiler_params=pltpu.CompilerParams(vmem_limit_bytes=VMEM_LIMIT),
-        cost_estimate=pl.CostEstimate(flops=2 * tokens * m * n, bytes_accessed=2 * tokens * (m + n) + 4 * m * n, transcendentals=0),
+        wgrad_kernel, grid=grid, out_shape=tuple(out_shapes), in_specs=specs, out_specs=tuple(out_specs),
+        compiler_params=pltpu.CompilerParams(vmem_limit_bytes=VMEM_LIMIT),
+        cost_estimate=pl.CostEstimate(flops=2 * units * tokens * dim * hid, bytes_accessed=2 * units * tokens * (dim + hid) + 4 * dim * hid,
+                                      transcendentals=0),
         name=name,
-    )(lhs, rhs)
-
-
-def place_kernel(dx, y, dx_out, y_out):
-    dx_out[...] = dx[...]
-    y_out[...] = y[...]
-
-
-def run_place(dx, y):
-    spec = pl.BlockSpec((1,) + dx.shape[1:], lambda i: (i, 0, 0))
-    shape = jax.ShapeDtypeStruct(dx.shape, BF16)
-    return pl.pallas_call(
-        place_kernel, grid=(dx.shape[0],), out_shape=(shape, shape), in_specs=[spec] * 2, out_specs=(spec, spec),
-        cost_estimate=pl.CostEstimate(flops=dx.size, bytes_accessed=8 * dx.size, transcendentals=0), name='place',
-    )(dx, y)
+    )(*operands)
 
 
 def solution(mesh):
@@ -719,12 +751,11 @@
 
     def local_fn(x, g, w_in, w_out):
         wi, wo = w_in[:, 0], w_out[:, 0]
-        hall, y, eall, gin_up, gout_up, _, _, alow, qlow, elow = run_front(stages, levels, x, g, wi, wo)
+        hall, y, eall, gin_up, gout_up, _, _, aqlow, elow = run_front(stages, levels, x, g, wi, wo)
         gin_up, gout_up = lax.psum((gin_up, gout_up), 'data')
-        alow, qlow, elow, dx, y = run_wide(stages, x.shape[0], hall, eall, y, alow, qlow, elow, wi, wo)
-        grad_in = run_wgrad(hall, qlow, False, 'gin_low')
-        grad_out = run_wgrad(alow, elow, True, 'gout_low')
-        dx, y = run_place(dx, y)
+        aqlow, elow, dx, y = run_wide(stages, x.shape[0], hall, eall, y, aqlow, elow, wi, wo)
+        grad_in, dx, y = run_wgrad(hall, aqlow, 1, False, (dx, y), 'gin_low')
+        grad_out, = run_wgrad(elow, aqlow, 0, True, (), 'gout_low')
         grad_in = lax.dynamic_update_slice(grad_in, gin_up[None], (1, 0, 0))
         grad_out = lax.dynamic_update_slice(grad_out, gout_up[None], (1, 0, 0))
         return y, dx, grad_in[:, None], grad_out[:, None]

time: 637 us -> 640 us (level)
    pallas_call x4 -> x3, Pallas kernels: 348 us -> 349 us  [the longest x1 250 us: run_wide(): pl.pallas_call(functools.partial(wide_kernel, stages, micros), out_shape=...]
where the time goes in v5:
time: 640 us
  Pallas kernels  613 us (96%)
  between operations  14.1 us (2%)
  local copies, waits for them, and re-layouts  13.1 us (2%)
    pallas_call x1, Pallas kernels, run_front(): pl.pallas_call(functools.partial(front_kernel, stages, levels, micros, ch...  264 us
    pallas_call x1, Pallas kernels, run_wide(): pl.pallas_call(functools.partial(wide_kernel, stages, micros), out_shape=...  250 us
    pallas_call x2, Pallas kernels, run_wgrad(): pl.pallas_call(wgrad_kernel, grid=grid, out_shape=tuple(out_shapes), in_s...  98.9 us
  transfers between devices with their start and end apart: 1, of which 0 were waited for; matrix products, arithmetic and copies ran while one was open for 0% of the time, Pallas kernels for 55%

profile of v5, /device:TPU:96, one launch (start us, length us, event | category | flops | bytes accessed | tf_op | source)
XLA Modules:
  0.0 640.2 jit_solution(10738700851297388525)
XLA Ops:
  7.2 0.1 all-reduce.3.cloned.1.call-start
  7.2 263.8 %front.1 = (bf16[32,256,768]{2,1,0:T(8,128)(2,1)}, bf16[8,256,768]{2,1,0:T(8,128)(2,1)}, bf16[32,256,768]{2,1,0:T(8,128)(2,1)}, f32[768,3072]{1,0:T(8,128)}, f32...) custom-call(bf16[8,256,768]{2,1,0:T(8,128)(2,1)} %x_hbm.1, ...), custom_call_target="tpu_custom_call" | custom-call | flops 86973087744 | bytes 50331648 | tf_op jit(solution)/shard_map/front/pallas_call | solution.py:476
  271.1 0.1 all-reduce.3.cloned.1.call-update
  271.1 250.2 %wide.1 = (bf16[32,2,256,3072]{3,2,1,0:T(8,128)(2,1)}, bf16[32,256,768]{2,1,0:T(8,128)(2,1)}, bf16[8,256,768]{2,1,0:T(8,128)(2,1)}, bf16[8,256,768]{2,1,0:T(8,128)(2,1)}) custom-call(bf16[32,256,768]{2,1,0:T(8,128)(2,1)} %get-tuple-element.18.hall.lhs, ...), custom_call_target="tpu_custom_call", output_to_operand_aliasing={{3}: (2, {}), {0}: (3, {}), {1}: (4, {})} | custom-call | flops 115964116992 | bytes 100663296 | tf_op jit(solution)/shard_map/wide/pallas_call | solution.py:684
  521.3 49.4 %gout_low.1 = f32[2,3072,768]{2,1,0:T(8,128)} custom-call(bf16[32,2,256,3072]{3,2,1,0:T(8,128)(2,1)} %get-tuple-element.23.rhs.lhs, bf16[32,256,768]{2,1,0:T(8,128)(2,1)} %get-tuple-element.30.rhs), custom_call_target="tpu_custom_call" | custom-call | flops 38654705664 | bytes 72351744 | tf_op jit(solution)/shard_map/gout_low/pallas_call | solution.py:740
  570.8 49.5 %gin_low.1 = (f32[2,768,3072]{2,1,0:T(8,128)}, bf16[8,256,768]{2,1,0:T(8,128)(2,1)}, bf16[8,256,768]{2,1,0:T(8,128)(2,1)}) custom-call(bf16[32,256,768]{2,1,0:T(8,128)(2,1)} %get-tuple-element.18.hall.lhs, bf16[32,2,256,3072]{3,2,1,0:T(8,128)(2,1)} %get-tuple-element.23.rhs.lhs, bf16[8,256,768]{2,1,0:T(8,128)(2,1)} %get-tuple-element.24.refs_0_, ...), custom_call_target="tpu_custom_call" | custom-call | flops 38654705664 | bytes 72351744 | tf_op jit(solution)/shard_map/gin_low/pallas_call | solution.py:740
  620.2 0.0 all-reduce.3.cloned.1.call-done
  620.3 0.0 slice-start
  620.3 0.0 slice-start.1
  620.3 0.0 slice-start.2
  620.3 8.7 %constant_dynamic-update-slice_fusion = f32[2,1,3072,768]{3,2,0,1:T(8,128)} fusion(f32[2,1,3072,768]{3,2,0,1:T(8,128)} %bitcast.14, f32[1,1,3072,768]{3,2,0,1:T(8,128)} %get-tuple-element.37), kind=kLoop, calls=%fused_computation | loop fusion | bytes 18874368 | tf_op jit(solution)/shard_map/dynamic_update_slice | solution.py:760
  629.0 0.0 slice-done
  629.0 0.0 slice-done.1
  629.0 0.0 slice-done.2
  629.0 4.4 constant_dynamic-update-slice_fusion.1
  (1 shorter events, 0.0 us)
Async XLA Ops:
  7.2 613.1 %all-reduce.3.cloned.1.call-start = ((), (), s32[]{:S(2)}) async-start(), calls=%async_computation | async-start | bytes 37748736 | tf_op jit(solution)/shard_map/psum | solution.py:755
  620.3 8.8 %slice-start = ((s8[9437184]{0:T(1024)(128)(4,1)}), s8[4194304]{0:T(1024)(128)(4,1)S(1)}, s32[]{:S(2)}) async-start(s8[9437184]{0:T(1024)(128)(4,1)} %bitcast.8), calls=%async_computation.1 | async-start | bytes 8388608
  620.3 8.7 %slice-start.1 = ((s8[9437184]{0:T(1024)(128)(4,1)}), s8[4194304]{0:T(1024)(128)(4,1)S(1)}, s32[]{:S(2)}) async-start(s8[9437184]{0:T(1024)(128)(4,1)} %bitcast.8), calls=%async_computation.2 | async-start | bytes 8388608
  620.3 8.7 %slice-start.2 = ((s8[9437184]{0:T(1024)(128)(4,1)}), s8[1048576]{0:T(1024)(128)(4,1)S(1)}, s32[]{:S(2)}) async-start(s8[9437184]{0:T(1024)(128)(4,1)} %bitcast.8), calls=%async_computation.3 | async-start | bytes 2097152
Sparse Core Ops, SparseCore 0:
  271.2 325.4 all-reduce.2

commit v6 on v5

--- a/solution.py
+++ b/solution.py
@@ -54,7 +54,7 @@
 
 
 def head_units(s, micros):
-    return jnp.minimum(jnp.maximum(s - 1, 0), micros // 2)
+    return jnp.minimum(jnp.maximum(s - 1, 0), 3 * micros // 8)
 
 
 def head_arrivals(s, stages, micros):
@@ -167,11 +167,6 @@
             src_ref=eall.at[(2 - j) * micros + m, rows], dst_ref=eall.at[3 * micros + m, rows], send_sem=e_send.at[2 + j, m],
             recv_sem=e_recv.at[2, m], device_id={'data': (up, down)[j]}, device_id_type=MESH)
 
-    def e_direct(m):
-        return pltpu.make_async_remote_copy(
-            src_ref=obuf.at[m], dst_ref=eall.at[3 * micros + m], send_sem=e_send.at[2, m], recv_sem=e_recv.at[2, m],
-            device_id={'data': lax.rem(d + 2, levels)}, device_id_type=MESH)
-
     def e_whole(m):
         return pltpu.make_async_remote_copy(
             src_ref=eall.at[m], dst_ref=eall.at[3 * micros + m], send_sem=e_send.at[2, m], recv_sem=e_recv.at[2, m],
@@ -185,6 +180,8 @@
 
     def loads(m):
         return (pltpu.make_async_copy(aup.at[m], abuf.at[1], a_load.at[0]), pltpu.make_async_copy(qup.at[m], qbuf.at[1], a_load.at[1]))
+
+    outs = (pltpu.make_async_copy(gin, gin_hbm, o_sem.at[0]), pltpu.make_async_copy(gout, gout_hbm, o_sem.at[1]))
 
     for v in range(2):
         for c in w_copies(v):
@@ -198,10 +195,9 @@
     def _():
         loop(0, micros, lambda m: g_copy(m).start())
 
-    signal_all([{'stage': lax.rem(s + step, stages)} for step in range(1, stages)] + [{'data': up}, {'data': down}, {'data': lax.rem(d + 2, levels)}])
-
-    for c in w_copies(0):
-        c.wait()
+    signal_all([{'stage': lax.rem(s + step, stages)} for step in range(1, stages)] + [{'data': up}, {'data': down}])
+
+    w_copies(0)[0].wait()
 
     def fwd_wait(i):
         lower = i < micros
@@ -242,6 +238,10 @@
             for cols in slices(hid, fb):
                 a[:, cols] = gelu_only(dot(hbuf[i], wi[v, :, cols])).astype(BF16)
 
+        @pl.when(i == 0)
+        def _():
+            w_copies(0)[1].wait()
+
         for cols in slices(dim, nb):
             out = hbuf[i, :, cols].astype(F32) + dot(a[...], wo[v, :, cols])
             obuf[o, :, cols] = out.astype(BF16)
@@ -305,10 +305,6 @@
             def _():
                 far(m - 1)
 
-            @pl.when(m == micros - 1)
-            def _():
-                e_direct(m).start()
-
         @pl.when(defer & upper)
         def _():
             q_keep(m).start()
@@ -327,6 +323,12 @@
     def weight_unit(m, k):
         for cols in slices(hid, wb):
             gin[:, cols] += dot_tn(hbuf[micros + m], qbuf[k, :, cols])
+
+        @pl.when(m == micros - 1)
+        def _():
+            outs[0].start()
+
+        for cols in slices(hid, wb):
             gout[cols, :] += dot_tn(abuf[k, :, cols], ebuf[m])
 
     def step(t):
@@ -402,9 +404,7 @@
 
     loop(0, 2 * micros + lag + jnp.where(defer, micros, heads), step)
 
-    outs = (pltpu.make_async_copy(gin, gin_hbm, o_sem.at[0]), pltpu.make_async_copy(gout, gout_hbm, o_sem.at[1]))
-    for c in outs:
-        c.start()
+    outs[1].start()
 
     def drain(m):
         h_keep(m).wait()
@@ -437,16 +437,15 @@
             e_keep(m).wait()
             for j in range(2):
                 e_push(m, j).wait_send()
-            e_whole(m).wait_recv()
 
             @pl.when(m < micros - 1)
             def _():
+                e_whole(m).wait_recv()
                 for j in range(2):
                     e_forward(m, j).wait_send()
 
             @pl.when(m == micros - 1)
             def _():
-                e_direct(m).wait_send()
                 for j in range(2):
                     e_push(m, j).wait_recv()
 
@@ -494,11 +493,13 @@
     )(x, g, w_in, w_out)
 
 
-def wide_kernel(stages, micros, hall, eall, _y, _aq, _e, wi_hbm, wo_hbm, aq_out, e_out, dx_out, y_out,
-                wi, wo, hbuf, obuf, ebuf, aqbuf,
-                w_sem, h_sem, n_send, b_send, b_recv, dx_sem, dx_send, dx_recv, y_send, y_recv, s_sem, k_sem, l_sem):
+def wide_kernel(stages, levels, micros, hall, eall, _y, _aq, _e, wi_hbm, wo_hbm, aq_out, e_out, dx_out, y_out,
+                wi, wo, hbuf, obuf, ebuf, nbuf, aqbuf,
+                w_sem, h_sem, n_send, b_send, b_recv, dx_sem, dx_send, dx_recv, y_send, y_recv, s_sem, k_sem, l_sem, n_sem, d_sem):
     s = lax.axis_index('stage')
+    d = lax.axis_index('data')
     nxt, prv = lax.rem(s + 1, stages), lax.rem(s + stages - 1, stages)
+    across = lax.rem(d + 2, levels)
     dim, hid = wi.shape
     units = ebuf.shape[0]
     fb = pick_block(hid, 768)
@@ -522,10 +523,18 @@
     def e_keep(i):
         return pltpu.make_async_copy(ebuf.at[i], e_out.at[i], l_sem.at[i])
 
+    def n_load(k):
+        return pltpu.make_async_copy(eall.at[part(k)], nbuf.at[part(k - 1)], n_sem.at[k - 1])
+
     def entry(i):
         return pltpu.make_async_remote_copy(
-            src_ref=eall.at[i], dst_ref=ebuf.at[i], send_sem=n_send.at[i], recv_sem=b_recv.at[i],
+            src_ref=nbuf.at[i - micros], dst_ref=ebuf.at[i], send_sem=n_send.at[i - micros], recv_sem=b_recv.at[i],
             device_id={'stage': prv}, device_id_type=MESH)
+
+    def entry_across():
+        return pltpu.make_async_remote_copy(
+            src_ref=eall.at[micros - 1], dst_ref=ebuf.at[units - 1], send_sem=d_sem, recv_sem=b_recv.at[units - 1],
+            device_id={'stage': prv, 'data': across}, device_id_type=MESH)
 
     def b_hop(i):
         o = lax.rem(i, micros)
@@ -581,11 +590,20 @@
         h_copy(k).start()
     loop(heads, arrivals, lambda i: e_load(i).start())
 
-    signal_all([{'stage': lax.rem(s + step, stages)} for step in range(1, stages)])
-
     @pl.when(first)
     def _():
-        loop(micros, units, lambda i: entry(i).start())
+        for k in range(1, groups):
+            n_load(k).start()
+
+    signal_all([{'stage': lax.rem(s + step, stages)} for step in range(1, stages)]
+               + [{'stage': st, 'data': across} for st in (nxt, prv)])
+
+    @pl.when(first)
+    def _():
+        entry_across().start()
+        for k in range(1, groups):
+            n_load(k).wait()
+            loop(k * micros, min((k + 1) * micros, units - 1), lambda i: entry(i).start())
 
     for c in w_copies:
         c.wait()
@@ -652,7 +670,8 @@
 
     @pl.when(first)
     def _():
-        loop(micros, units, lambda i: entry(i).wait_send())
+        loop(micros, units - 1, lambda i: entry(i).wait_send())
+        entry_across().wait_send()
         loop(0, micros, lambda m: dx_copy(m).wait())
 
     @pl.when(jnp.logical_not(first))
@@ -674,7 +693,7 @@
         e_part(k).wait()
 
 
-def run_wide(stages, micros, hall, eall, y, aqlow, elow, w_in, w_out):
+def run_wide(stages, levels, micros, hall, eall, y, aqlow, elow, w_in, w_out):
     units, tokens, dim = hall.shape
     _, _, hid = w_in.shape
     groups = units // micros
@@ -682,15 +701,15 @@
     small = jax.ShapeDtypeStruct((micros, tokens, dim), BF16)
     acts = jax.ShapeDtypeStruct((units, 2, tokens, hid), BF16)
     return pl.pallas_call(
-        functools.partial(wide_kernel, stages, micros),
+        functools.partial(wide_kernel, stages, levels, micros),
         out_shape=(acts, jax.ShapeDtypeStruct((units, tokens, dim), BF16), small, small),
         in_specs=[ANY] * 7, out_specs=(ANY,) * 4,
         scratch_shapes=[
             pltpu.VMEM((dim, hid), BF16), pltpu.VMEM((hid, dim), BF16),
             pltpu.VMEM((units, tokens, dim), BF16), pltpu.VMEM((micros, tokens, dim), BF16), pltpu.VMEM((units, tokens, dim), BF16),
-            pltpu.VMEM((2, 2, tokens, hid), BF16),
-            dma((2,)), dma((groups,)), dma((units,)), dma((micros,)), dma((units,)), dma((micros,)), dma((micros,)), dma((micros,)),
-            dma((micros,)), dma((micros,)), dma((2,)), dma((groups,)), dma((micros,)),
+            pltpu.VMEM((units - micros, tokens, dim), BF16), pltpu.VMEM((2, 2, tokens, hid), BF16),
+            dma((2,)), dma((groups,)), dma((units - micros,)), dma((micros,)), dma((units,)), dma((micros,)), dma((micros,)), dma((micros,)),
+            dma((micros,)), dma((micros,)), dma((2,)), dma((groups,)), dma((micros,)), dma((groups - 1,)), dma,
         ],
         input_output_aliases={2: 3, 3: 0, 4: 1},
         compiler_params=pltpu.CompilerParams(collective_id=1, has_side_effects=True, vmem_limit_bytes=VMEM_LIMIT),
@@ -753,7 +772,7 @@
         wi, wo = w_in[:, 0], w_out[:, 0]
         hall, y, eall, gin_up, gout_up, _, _, aqlow, elow = run_front(stages, levels, x, g, wi, wo)
         gin_up, gout_up = lax.psum((gin_up, gout_up), 'data')
-        aqlow, elow, dx, y = run_wide(stages, x.shape[0], hall, eall, y, aqlow, elow, wi, wo)
+        aqlow, elow, dx, y = run_wide(stages, levels, x.shape[0], hall, eall, y, aqlow, elow, wi, wo)
         grad_in, dx, y = run_wgrad(hall, aqlow, 1, False, (dx, y), 'gin_low')
         grad_out, = run_wgrad(elow, aqlow, 0, True, (), 'gout_low')
         grad_in = lax.dynamic_update_slice(grad_in, gin_up[None], (1, 0, 0))

time: 640 us -> 641 us (level)
  no operation moved by 1% of the time
where the time goes in v6:
time: 641 us
  Pallas kernels  614 us (96%)
  between operations  14.1 us (2%)
  local copies, waits for them, and re-layouts  13.1 us (2%)
    pallas_call x1, Pallas kernels, run_front(): pl.pallas_call(functools.partial(front_kernel, stages, levels, micros, ch...  260 us
    pallas_call x1, Pallas kernels, run_wide(): pl.pallas_call(functools.partial(wide_kernel, stages, levels, micros), ou...  255 us
    pallas_call x2, Pallas kernels, run_wgrad(): pl.pallas_call(wgrad_kernel, grid=grid, out_shape=tuple(out_shapes), in_s...  98.9 us
  transfers between devices with their start and end apart: 1, of which 0 were waited for; matrix products, arithmetic and copies ran while one was open for 0% of the time, Pallas kernels for 55%

profile of v6, /device:TPU:96, one launch (start us, length us, event | category | flops | bytes accessed | tf_op | source)
XLA Modules:
  0.0 641.3 jit_solution(9885044164076042980)
XLA Ops:
  7.2 0.1 all-reduce.3.cloned.1.call-start
  7.2 259.7 %front.1 = (bf16[32,256,768]{2,1,0:T(8,128)(2,1)}, bf16[8,256,768]{2,1,0:T(8,128)(2,1)}, bf16[32,256,768]{2,1,0:T(8,128)(2,1)}, f32[768,3072]{1,0:T(8,128)}, f32...) custom-call(bf16[8,256,768]{2,1,0:T(8,128)(2,1)} %x_hbm.1, ...), custom_call_target="tpu_custom_call" | custom-call | flops 86973087744 | bytes 50331648 | tf_op jit(solution)/shard_map/front/pallas_call | solution.py:475
  266.9 0.1 all-reduce.3.cloned.1.call-update
  267.0 255.4 %wide.1 = (bf16[32,2,256,3072]{3,2,1,0:T(8,128)(2,1)}, bf16[32,256,768]{2,1,0:T(8,128)(2,1)}, bf16[8,256,768]{2,1,0:T(8,128)(2,1)}, bf16[8,256,768]{2,1,0:T(8,128)(2,1)}) custom-call(bf16[32,256,768]{2,1,0:T(8,128)(2,1)} %get-tuple-element.18.hall.lhs, ...), custom_call_target="tpu_custom_call", output_to_operand_aliasing={{3}: (2, {}), {0}: (3, {}), {1}: (4, {})} | custom-call | flops 115964116992 | bytes 100663296 | tf_op jit(solution)/shard_map/wide/pallas_call | solution.py:703
  522.4 49.4 %gout_low.1 = f32[2,3072,768]{2,1,0:T(8,128)} custom-call(bf16[32,2,256,3072]{3,2,1,0:T(8,128)(2,1)} %get-tuple-element.23.rhs.lhs, bf16[32,256,768]{2,1,0:T(8,128)(2,1)} %get-tuple-element.30.rhs), custom_call_target="tpu_custom_call" | custom-call | flops 38654705664 | bytes 72351744 | tf_op jit(solution)/shard_map/gout_low/pallas_call | solution.py:759
  571.8 49.5 %gin_low.1 = (f32[2,768,3072]{2,1,0:T(8,128)}, bf16[8,256,768]{2,1,0:T(8,128)(2,1)}, bf16[8,256,768]{2,1,0:T(8,128)(2,1)}) custom-call(bf16[32,256,768]{2,1,0:T(8,128)(2,1)} %get-tuple-element.18.hall.lhs, bf16[32,2,256,3072]{3,2,1,0:T(8,128)(2,1)} %get-tuple-element.23.rhs.lhs, bf16[8,256,768]{2,1,0:T(8,128)(2,1)} %get-tuple-element.24.refs_0_, ...), custom_call_target="tpu_custom_call" | custom-call | flops 38654705664 | bytes 72351744 | tf_op jit(solution)/shard_map/gin_low/pallas_call | solution.py:759
  621.3 0.0 all-reduce.3.cloned.1.call-done
  621.3 0.0 slice-start
  621.3 0.0 slice-start.1
  621.3 0.0 slice-start.2
  621.3 8.7 %constant_dynamic-update-slice_fusion = f32[2,1,3072,768]{3,2,0,1:T(8,128)} fusion(f32[2,1,3072,768]{3,2,0,1:T(8,128)} %bitcast.14, f32[1,1,3072,768]{3,2,0,1:T(8,128)} %get-tuple-element.37), kind=kLoop, calls=%fused_computation | loop fusion | bytes 18874368 | tf_op jit(solution)/shard_map/dynamic_update_slice | solution.py:779
  630.1 0.0 slice-done
  630.1 0.0 slice-done.1
  630.1 0.0 slice-done.2
  630.1 4.4 constant_dynamic-update-slice_fusion.1
  (1 shorter events, 0.0 us)
Async XLA Ops:
  7.2 614.1 %all-reduce.3.cloned.1.call-start = ((), (), s32[]{:S(2)}) async-start(), calls=%async_computation | async-start | bytes 37748736 | tf_op jit(solution)/shard_map/psum | solution.py:774
  621.3 8.8 %slice-start = ((s8[9437184]{0:T(1024)(128)(4,1)}), s8[4194304]{0:T(1024)(128)(4,1)S(1)}, s32[]{:S(2)}) async-start(s8[9437184]{0:T(1024)(128)(4,1)} %bitcast.8), calls=%async_computation.1 | async-start | bytes 8388608
  621.3 8.7 %slice-start.1 = ((s8[9437184]{0:T(1024)(128)(4,1)}), s8[4194304]{0:T(1024)(128)(4,1)S(1)}, s32[]{:S(2)}) async-start(s8[9437184]{0:T(1024)(128)(4,1)} %bitcast.8), calls=%async_computation.2 | async-start | bytes 8388608
  621.3 8.7 %slice-start.2 = ((s8[9437184]{0:T(1024)(128)(4,1)}), s8[1048576]{0:T(1024)(128)(4,1)S(1)}, s32[]{:S(2)}) async-start(s8[9437184]{0:T(1024)(128)(4,1)} %bitcast.8), calls=%async_computation.3 | async-start | bytes 2097152
Sparse Core Ops, SparseCore 0:
  267.1 324.4 all-reduce.2
